TPU v7x, 32 devices: a whole 2x2x4 slice. The times are simulated.
32 devices in a mesh: gx: 8 (over z, x), ma: 4 (over y, core).
Axes of the slice: x: 2, y: 2, z: 4, core: 2. Of those that a mesh axis runs over, the one named last changes fastest.
Arguments:
- recorded: float32 [4096, 128, 128], P('ma', 'gx'), may hold values from -51 to 51
- kernel: bfloat16 [2, 8, 4096, 4096], P(None, 'gx', 'ma'), may hold values from -1 to 1
- freq_bins: int32 [8], replicated, may hold values from 1 to 63
- window_start: int32 [4096, 128], P('ma', 'gx'), may hold values from 0 to 31
- window_stop: int32 [4096, 128], P('ma', 'gx'), may hold values from 97 to 128
Outputs:
- solution: float32 [4096, 128, 128], P('ma', 'gx')
- residual: float32 [4096, 128, 128], P('ma', 'gx')
- direction: float32 [4096, 128, 128], P('ma', 'gx')
All inputs are finite; a program needn't handle non-finite values.
Results may differ from a plain program's by a relative error of at most 0.015.
Values may be sent and summed in bfloat16 or wider, within the bound.
A program may use at most 128 MiB of HBM per device.

v0:
```python
import functools
import math

import jax
import jax.numpy as jnp
from jax import lax
from jax.experimental import pallas as pl
from jax.experimental.pallas import tpu as pltpu
from jax.sharding import PartitionSpec as P

RAMP = 8
MESH = pl.DeviceIdType.MESH

epsilon = 1e-06


def phase_table(freq_bins, length):
    samples = jnp.arange(length, dtype=jnp.int32)
    angles = (freq_bins[:, None] * samples[None, :] % length).astype(jnp.float32) * (
        2.0 * math.pi / length
    )
    return jnp.stack([jnp.cos(angles), -jnp.sin(angles)], 1) * math.sqrt(2.0 / length)


def taper_weights(window_start, window_stop, length):
    samples = jnp.arange(length, dtype=jnp.float32)
    rising = jnp.clip(
        (samples[None, None, :] - window_start[:, :, None].astype(jnp.float32) + 1.0) / RAMP,
        0.0,
        1.0,
    )
    falling = jnp.clip(
        (window_stop[:, :, None].astype(jnp.float32) - samples[None, None, :]) / RAMP, 0.0, 1.0
    )
    return rising * falling


def exchange_kernel(n, x_ref, o_ref, send_sem, recv_sem, own_sem):
    me = lax.axis_index("gx")
    barrier = pltpu.get_barrier_semaphore()
    for k in range(1, n):
        pl.semaphore_signal(
            barrier, inc=1, device_id={"gx": lax.rem(me + k, n)}, device_id_type=MESH
        )
    own = pltpu.make_async_copy(x_ref.at[me], o_ref.at[me], own_sem)
    own.start()
    pl.semaphore_wait(barrier, n - 1)
    copies = []
    for k in range(1, n):
        peer = lax.rem(me + k, n)
        copy = pltpu.make_async_remote_copy(
            src_ref=x_ref.at[peer],
            dst_ref=o_ref.at[me],
            send_sem=send_sem.at[k],
            recv_sem=recv_sem.at[k],
            device_id={"gx": peer},
            device_id_type=MESH,
        )
        copy.start()
        copies.append(copy)
    own.wait()
    for copy in copies:
        copy.wait()


def exchange(x, n, number):
    return pl.pallas_call(
        functools.partial(exchange_kernel, n),
        out_shape=jax.ShapeDtypeStruct(x.shape, x.dtype),
        in_specs=[pl.BlockSpec(memory_space=pltpu.VMEM)],
        out_specs=pl.BlockSpec(memory_space=pltpu.VMEM),
        scratch_shapes=[
            pltpu.SemaphoreType.DMA((n,)),
            pltpu.SemaphoreType.DMA((n,)),
            pltpu.SemaphoreType.DMA,
        ],
        compiler_params=pltpu.CompilerParams(collective_id=number, has_side_effects=True),
        name=f"exchange{number}",
    )(x)


def total_kernel(outer, inner, x_ref, o_ref, held, send_sem, recv_sem):
    n = outer * inner
    me = lax.axis_index("gx") * inner + lax.axis_index("ma")
    barrier = pltpu.get_barrier_semaphore()

    def place(k):
        peer = lax.rem(me + k, n)
        return (peer // inner, lax.rem(peer, inner))

    for k in range(1, n):
        pl.semaphore_signal(barrier, inc=1, device_id=place(k), device_id_type=MESH)
    pl.semaphore_wait(barrier, n - 1)
    copies = []
    for k in range(1, n):
        copy = pltpu.make_async_remote_copy(
            src_ref=x_ref,
            dst_ref=held.at[me],
            send_sem=send_sem.at[k],
            recv_sem=recv_sem.at[k],
            device_id=place(k),
            device_id_type=MESH,
        )
        copy.start()
        copies.append(copy)
    held[me] = x_ref[...]
    for copy in copies:
        copy.wait()
    o_ref[...] = jnp.sum(held[...], axis=0)


def total(x, outer, inner, number):
    n = outer * inner
    return pl.pallas_call(
        functools.partial(total_kernel, outer, inner),
        out_shape=jax.ShapeDtypeStruct(x.shape, x.dtype),
        in_specs=[pl.BlockSpec(memory_space=pltpu.VMEM)],
        out_specs=pl.BlockSpec(memory_space=pltpu.VMEM),
        scratch_shapes=[
            pltpu.VMEM((n,) + x.shape, x.dtype),
            pltpu.SemaphoreType.DMA((n,)),
            pltpu.SemaphoreType.DMA((n,)),
        ],
        compiler_params=pltpu.CompilerParams(collective_id=number, has_side_effects=True),
        name=f"total{number}",
    )(x)


def pairs(n, bit):
    return [(i, i ^ bit) for i in range(n)]


def scatter_sum(partial, n):
    rows, block = partial.shape[1:]
    me = lax.axis_index("ma")
    held = partial
    bit = 1
    while bit < n:
        own = (me // bit) % 2
        parts = held.reshape(-1, 2, rows, block)
        keep = lax.dynamic_index_in_dim(parts, own, 1, keepdims=False)
        send = lax.dynamic_index_in_dim(parts, 1 - own, 1, keepdims=False)
        got = lax.ppermute(send, "ma", pairs(n, bit))
        held = (keep.astype(jnp.float32) + got.astype(jnp.float32)).astype(jnp.bfloat16)
        bit *= 2
    return held.reshape(rows, block)


def gather_all(x, n):
    rows, block = x.shape
    me = lax.axis_index("ma")
    held = x.reshape(rows, 1, block)
    bit = n // 2
    while bit >= 1:
        own = (me // bit) % 2
        got = lax.ppermute(held, "ma", pairs(n, bit))
        first = jnp.where(own == 0, held, got)
        second = jnp.where(own == 0, got, held)
        held = jnp.stack([first, second], 2).reshape(rows, -1, block)
        bit //= 2
    return held.reshape(rows, n * block)


def to_spectra(traces, table):
    freqs = table.shape[0]
    flat = table.reshape(2 * freqs, table.shape[2]).astype(jnp.bfloat16)
    out = jnp.einsum(
        "ast,kt->ksa", traces.astype(jnp.bfloat16), flat, preferred_element_type=jnp.float32
    ).astype(jnp.bfloat16)
    return out.reshape(freqs, 2 * out.shape[1], out.shape[2])


def to_traces(spectra, table):
    freqs, double, points = spectra.shape
    sources = double // 2
    length = table.shape[2]
    depth = freqs * double
    across = spectra.reshape(depth, points).T
    owner = jnp.arange(depth, dtype=jnp.int32) % sources
    mask = (owner[None, :] == jnp.arange(sources, dtype=jnp.int32)[:, None]).astype(jnp.bfloat16)
    spread = (across[:, None, :] * mask[None]).reshape(points * sources, depth)
    tall = jnp.repeat(table.reshape(2 * freqs, length).astype(jnp.bfloat16), sources, axis=0)
    out = jnp.dot(spread, tall, preferred_element_type=jnp.float32)
    return out.reshape(points, sources, length)


def by_frequency(arrived, n):
    sources = arrived.shape[1] // 2
    points = arrived.shape[2]
    return arrived.reshape(n, 2, sources, points).transpose(1, 0, 2, 3).reshape(2, -1, points)


def by_source(spectra, n):
    points = spectra.shape[2]
    sources = spectra.shape[1] // n
    return spectra.reshape(2, n, sources, points).transpose(1, 0, 2, 3).reshape(n, -1, points)


def adjoint_kernel(d_ref, k_ref, o_ref):
    half = d_ref.shape[0] // 2
    data = d_ref[...]
    first = jnp.dot(data, k_ref[0], preferred_element_type=jnp.float32)
    second = jnp.dot(data, k_ref[1], preferred_element_type=jnp.float32)
    o_ref[0, :half] = (first[:half] + second[half:]).astype(o_ref.dtype)
    o_ref[0, half:] = (first[half:] - second[:half]).astype(o_ref.dtype)


def adjoint_product(data, flat_kernel, inner):
    sources, rows = data.shape[1], data.shape[2]
    columns = flat_kernel.shape[1]
    block = columns // inner
    tile = min(512, block)
    per_block = block // tile
    partial = pl.pallas_call(
        adjoint_kernel,
        grid=(columns // tile,),
        out_shape=jax.ShapeDtypeStruct((inner, 2 * sources, block), jnp.bfloat16),
        in_specs=[
            pl.BlockSpec((2 * sources, rows), lambda j: (0, 0)),
            pl.BlockSpec((2, rows, tile), lambda j: (0, 0, j)),
        ],
        out_specs=pl.BlockSpec(
            (1, 2 * sources, tile), lambda j: (j // per_block, 0, j % per_block)
        ),
        compiler_params=pltpu.CompilerParams(vmem_limit_bytes=60 * 1024 * 1024),
        cost_estimate=pl.CostEstimate(
            flops=8 * sources * rows * columns,
            bytes_accessed=4 * rows * columns + 4 * sources * (rows + columns),
            transcendentals=0,
        ),
        name="adjoint",
    )(data.reshape(2 * sources, rows), flat_kernel.reshape(2, rows, columns))
    return scatter_sum(partial, inner).reshape(2, sources, block)


def final_kernel(
    sums_ref, rec_ref, win_ref, g_ref, d_ref, h_ref, tall_ref, mask_ref, pick_ref,
    sol_ref, res_ref, dir_ref,
):
    tile, sources, length = rec_ref.shape
    norm_start, norm_data = sums_ref[0, 0], sums_ref[1, 0]
    cross, norm_change = sums_ref[2, 0], sums_ref[3, 0]
    step_size = norm_start / (norm_data + epsilon)
    norm_final = norm_start - 2.0 * step_size * cross + step_size * step_size * norm_change
    ratio = norm_final / (norm_start + epsilon)
    tall = tall_ref[...]

    def rows(values, mask):
        return (values[:, None, :] * mask[None]).reshape(tile * sources, -1).astype(jnp.bfloat16)

    def traces(ref):
        spread = rows(ref[...].astype(jnp.float32), mask_ref[...])
        out = jnp.dot(spread, tall, preferred_element_type=jnp.float32)
        return out.reshape(tile, sources, length)

    gradient = traces(g_ref)
    change = traces(h_ref)
    sol_ref[...] = step_size * gradient
    dir_ref[...] = (gradient - step_size * change) + ratio * gradient
    window = win_ref[...]
    ones = jnp.ones((window.shape[1], length), jnp.bfloat16)
    shape = (tile, sources, length)
    start = jnp.dot(rows(window, pick_ref[0]), ones, preferred_element_type=jnp.float32)
    stop = jnp.dot(rows(window, pick_ref[1]), ones, preferred_element_type=jnp.float32)
    samples = lax.broadcasted_iota(jnp.int32, shape, 2).astype(jnp.float32)
    rising = jnp.clip((samples - start.reshape(shape) + 1.0) / RAMP, 0.0, 1.0)
    falling = jnp.clip((stop.reshape(shape) - samples) / RAMP, 0.0, 1.0)
    image = (rising * falling) * traces(d_ref)
    res_ref[...] = rec_ref[...] - step_size * image


def final_step(sums, recorded, window_start, window_stop, returned, arrived, changed, table):
    points, sources, length = recorded.shape
    depth = returned.shape[0] * returned.shape[1]
    tile = min(128, points)

    def across(x):
        return x.reshape(depth, points).T

    place = jnp.arange(sources, dtype=jnp.int32)
    owner = jnp.arange(depth, dtype=jnp.int32) % sources
    mask = (owner[None, :] == place[:, None]).astype(jnp.float32)
    column = jnp.arange(2 * sources, dtype=jnp.int32)
    pick = jnp.stack(
        [column[None, :] == place[:, None], column[None, :] == place[:, None] + sources]
    ).astype(jnp.float32)
    tall = jnp.repeat(table.reshape(-1, length).astype(jnp.bfloat16), sources, axis=0)
    window = jnp.concatenate([window_start, window_stop], 1).astype(jnp.float32)
    whole3 = pl.BlockSpec((tile, sources, length), lambda i: (i, 0, 0))
    strip = pl.BlockSpec((tile, depth), lambda i: (i, 0))
    return pl.pallas_call(
        final_kernel,
        grid=(points // tile,),
        out_shape=[jax.ShapeDtypeStruct(recorded.shape, jnp.float32)] * 3,
        in_specs=[
            pl.BlockSpec(memory_space=pltpu.SMEM),
            whole3,
            pl.BlockSpec((tile, 2 * sources), lambda i: (i, 0)),
            strip,
            strip,
            strip,
            pl.BlockSpec((depth, length), lambda i: (0, 0)),
            pl.BlockSpec((sources, depth), lambda i: (0, 0)),
            pl.BlockSpec((2, sources, 2 * sources), lambda i: (0, 0, 0)),
        ],
        out_specs=[whole3] * 3,
        compiler_params=pltpu.CompilerParams(vmem_limit_bytes=48 * 1024 * 1024),
        cost_estimate=pl.CostEstimate(
            flops=8 * points * sources * depth * length,
            bytes_accessed=16 * points * sources * length,
            transcendentals=0,
        ),
        name="final",
    )(sums, recorded, window, across(returned), across(arrived), across(changed), tall, mask, pick)


def forward_product(model, flat_kernel, inner):
    sources = model.shape[1]
    incoming = gather_all(model.reshape(2 * sources, -1), inner)
    product = lax.dot_general(
        incoming, flat_kernel, (((1,), (1,)), ((), ())), preferred_element_type=jnp.float32
    )
    half = flat_kernel.shape[0] // 2
    real_part = product[:sources, :half] - product[sources:, half:]
    imaginary = product[sources:, :half] + product[:sources, half:]
    return jnp.stack([real_part, imaginary], 0).astype(jnp.bfloat16)


def per_device(outer, inner, recorded, kernel, freq_bins, window_start, window_stop):
    length = recorded.shape[2]
    table = phase_table(freq_bins, length)
    weights = taper_weights(window_start, window_stop, length)
    flat_kernel = kernel.reshape(2 * kernel.shape[2], kernel.shape[3])

    data = by_frequency(exchange(to_spectra(weights * recorded, table), outer, 0), outer)
    adjoint = adjoint_product(data, flat_kernel, inner)
    returned = lax.all_to_all(
        by_source(adjoint, outer), "gx", split_axis=0, concat_axis=0, tiled=True
    )

    same = freq_bins[:, None] == freq_bins[None, :]
    repeated = jnp.sum(same.astype(jnp.int32)) > freq_bins.shape[0]

    def combined(spectra):
        parts = lax.all_to_all(
            by_source(spectra, outer), "gx", split_axis=0, concat_axis=0, tiled=True
        )
        mixed = jnp.einsum(
            "gf,fxa->gxa",
            same.astype(jnp.bfloat16),
            parts,
            preferred_element_type=jnp.float32,
        ).astype(jnp.bfloat16)
        back = lax.all_to_all(mixed, "gx", split_axis=0, concat_axis=0, tiled=True)
        return by_frequency(back, outer)

    model = lax.cond(repeated, combined, lambda spectra: spectra, adjoint)
    outgoing = by_source(forward_product(model, flat_kernel, inner), outer)
    imaged = exchange(outgoing, outer, 1)
    image = weights * to_traces(imaged, table)
    second = by_frequency(exchange(to_spectra(weights * image, table), outer, 2), outer)
    normal = adjoint_product(second, flat_kernel, inner)
    changed = exchange(by_source(normal, outer), outer, 3)

    double, points = returned.shape[1:]
    depth = freq_bins.shape[0] * double
    eye = jnp.eye(double, dtype=jnp.bfloat16)
    mixing = (same.astype(jnp.bfloat16)[:, None, :, None] * eye[None, :, None, :]).reshape(
        depth, depth
    )
    flat_g = returned.reshape(depth, points)
    flat_h = changed.reshape(depth, points)
    mixed_g = jnp.dot(mixing, flat_g, preferred_element_type=jnp.float32)
    mixed_h = jnp.dot(mixing, flat_h, preferred_element_type=jnp.float32)
    sums = jnp.stack(
        [
            jnp.sum(flat_g.astype(jnp.float32) * mixed_g),
            jnp.sum(image * image),
            jnp.sum(mixed_g * flat_h.astype(jnp.float32)),
            jnp.sum(flat_h.astype(jnp.float32) * mixed_h),
        ]
    )
    sums = total(jnp.broadcast_to(jnp.tile(sums, 2)[:, None], (8, 128)), outer, inner, 4)
    if recorded.shape[1] % 8 == 0:
        return tuple(
            final_step(
                sums, recorded, window_start, window_stop, returned, imaged, changed, table
            )
        )
    gradient = to_traces(returned, table)
    change = to_traces(changed, table)
    norm_start, norm_data, cross, norm_change = sums[0, 0], sums[1, 0], sums[2, 0], sums[3, 0]
    step_size = norm_start / (norm_data + epsilon)
    norm_final = norm_start - 2.0 * step_size * cross + step_size * step_size * norm_change
    solution = step_size * gradient
    residual = recorded - step_size * image
    direction = gradient - step_size * change + norm_final / (norm_start + epsilon) * gradient
    return (solution, residual, direction)


def solution(mesh):
    in_specs = (P("ma", "gx", None), P(None, "gx", "ma", None), P(), P("ma", "gx"), P("ma", "gx"))
    out_specs = (P("ma", "gx", None), P("ma", "gx", None), P("ma", "gx", None))
    return jax.shard_map(
        functools.partial(per_device, mesh.shape["gx"], mesh.shape["ma"]),
        mesh=mesh,
        in_specs=in_specs,
        out_specs=out_specs,
        check_vma=False,
    )
```

profile of v0, /device:TPU:0, one launch (start us, length us, event | category | flops | bytes accessed | tf_op | source)
XLA Modules:
  0.0 237.0 jit_solution(6633918178760804108)
XLA Ops:
  0.6 0.8 fusion.36
  1.4 0.8 convert_element_type.148
  2.3 0.8 convert_element_type.149
  3.1 7.4 %fusion.18 = bf16[16,16,1024]{2,0,1:T(8,128)(2,1)S(1)} fusion(bf16[16,128,1]{1,0,2:T(8,128)(2,1)S(1)} %bitcast.141, f32[1024,16,128]{2,1,0:T(8,128)} %rec_ref.1, f32[1024,16]{0,1:T(8,128)S(1)} %convert_element_type.149, f32[1024,16]{0,1:T(8,128)S(1)} %convert_element_type.148), kind=kOutput, calls=%fused_computation.24 | convolution fusion | flops 88342528 | bytes 9048064 | tf_op jit(solution)/shard_map/ast,kt->ksa/dot_general | solution.py:167
  10.5 1.1 copy.132
  11.6 16.4 %exchange0.1 = bf16[8,32,1024]{2,1,0:T(8,128)(2,1)} custom-call(bf16[8,32,1024]{2,1,0:T(8,128)(2,1)} %bitcast.131), custom_call_target="tpu_custom_call" | custom-call | tf_op jit(solution)/shard_map/exchange0/pallas_call | solution.py:67
  28.0 1.9 copy.133
  29.9 11.6 %adjoint.2 = bf16[4,256,1024]{2,1,0:T(8,128)(2,1)} custom-call(bf16[256,1024]{1,0:T(8,128)(2,1)} %bitcast.121, bf16[2,1024,4096]{2,1,0:T(8,128)(2,1)} %bitcast.111), custom_call_target="tpu_custom_call" | custom-call | flops 4294967296 | bytes 19398656 | tf_op jit(solution)/shard_map/adjoint/pallas_call | solution.py:214
  41.5 1.3 dynamic-slice_bitcast_fusion.1
  42.8 0.1 collective-permute-start
  42.9 2.6 %collective-permute-done = bf16[2,256,1024]{2,1,0:T(8,128)(2,1)S(1)} collective-permute-done((bf16[2,256,1024]{2,1,0:T(8,128)(2,1)S(1)}, bf16[2,256,1024]{2,1,0:T(8,128)(2,1)S(1)}, u32[]{:S(2)}, u32[]{:S(2)}) %collective-permute-start) | collective-permute-done | bytes 1048608 | tf_op jit(solution)/shard_map/ppermute | solution.py:143
  45.5 1.6 fusion.13
  47.2 1.6 collective-permute-start.1
  48.8 0.7 convert_reduce_fusion
  50.1 0.1 broadcast_compare_fusion
  50.2 11.0 %collective-permute-done.1 = bf16[1,256,1024]{2,1,0:T(8,128)(2,1)S(1)} collective-permute-done((bf16[1,256,1024]{2,1,0:T(8,128)(2,1)S(1)}, bf16[1,256,1024]{2,1,0:T(8,128)(2,1)S(1)}, u32[]{:S(2)}, u32[]{:S(2)}) %collective-permute-start.1) | collective-permute-done | bytes 524320 | tf_op jit(solution)/shard_map/ppermute | solution.py:143
  61.2 0.2 add_convert_fusion.1
  61.4 0.2 conditional.1
  61.7 1.6 collective-permute-start.2
  63.3 11.6 %collective-permute-done.2 = bf16[256,1,1024]{2,0,1:T(8,128)(2,1)S(1)} collective-permute-done((bf16[256,1,1024]{2,0,1:T(8,128)(2,1)S(1)}, bf16[256,1,1024]{2,0,1:T(8,128)(2,1)S(1)}, u32[]{:S(2)}, u32[]{:S(2)}) %collective-permute-start.2) | collective-permute-done | bytes 524320 | tf_op jit(solution)/shard_map/ppermute | solution.py:156
  74.9 0.1 select_bitcast_fusion.3
  74.9 1.1 maximum_bitcast_fusion
  76.0 0.0 collective-permute-start.3
  76.0 2.9 %collective-permute-done.3 = bf16[256,2,1024]{2,0,1:T(8,128)(2,1)S(1)} collective-permute-done((bf16[256,2,1024]{2,0,1:T(8,128)(2,1)}, bf16[256,2,1024]{2,0,1:T(8,128)(2,1)S(1)}, u32[]{:S(2)}, u32[]{:S(2)}) %collective-permute-start.3) | collective-permute-done | bytes 1048608 | tf_op jit(solution)/shard_map/ppermute | solution.py:156
  78.9 0.1 select_bitcast_fusion.1
  79.0 0.2 pad_maximum_fusion
  79.2 2.6 %copy.136 = bf16[256,2,2,1024]{0,3,2,1:T(8,128)(2,1)} copy(bf16[256,2,2,1024]{3,0,1,2:T(8,128)(2,1)S(1)} %pad_maximum_fusion) | data formatting | bytes 4194304 | tf_op jit(solution)/shard_map/stack | solution.py:159
  81.8 8.8 %fusion.43 = f32[256,2048]{1,0:T(8,128)S(1)} fusion(bf16[256,4096]{0,1:T(8,128)(2,1)} %bitcast.124, bf16[2048,4096]{1,0:T(8,128)(2,1)} %bitcast.112), kind=kOutput, calls=%fused_computation.80 | convolution fusion | flops 4294967296 | bytes 20971520 | tf_op jit(solution)/shard_map/dot_general | solution.py:320
  90.6 0.1 fusion.25
  90.7 0.8 pad_maximum_fusion.1
  91.5 17.8 %exchange1.1 = bf16[8,32,1024]{2,1,0:T(8,128)(2,1)} custom-call(bf16[8,32,1024]{2,1,0:T(8,128)(2,1)} %bitcast.130), custom_call_target="tpu_custom_call" | custom-call | tf_op jit(solution)/shard_map/exchange1/pallas_call | solution.py:67
  109.3 1.2 copy.139
  110.6 5.3 %multiply_reduce_fusion = (f32[]{:T(128)}, f32[1024,16,128]{2,0,1:T(8,128)S(1)}) fusion(f32[1024,16]{0,1:T(8,128)S(1)} %convert_element_type.149, f32[1024,16]{0,1:T(8,128)S(1)} %convert_element_type.148, bf16[256,128,1]{1,0,2:T(8,128)(2,1)S(1)} %bitcast.109, bf16[16,256]{1,0:T(8,128)(2,1)S(1)} %get-tuple-element.25, bf16[1024,256]{1,0:T(8,128)(2,1)S(1)} %bitcast.105), kind=kOutput, calls=%fused_computation.6 | convolution fusion | flops 1101004800 | bytes 9117700 | tf_op jit(solution)/shard_map/dot_general | solution.py:183
  115.9 7.5 %fusion.21 = bf16[16,16,1024]{2,0,1:T(8,128)(2,1)S(1)} fusion(bf16[16,128,1]{1,0,2:T(8,128)(2,1)S(1)} %bitcast.143, f32[1024,16]{0,1:T(8,128)S(1)} %convert_element_type.149, f32[1024,16]{0,1:T(8,128)S(1)} %convert_element_type.148, f32[1024,16,128]{2,0,1:T(8,128)S(1)} %get-tuple-element.31), kind=kOutput, calls=%fused_computation.25 | convolution fusion | flops 90439680 | bytes 9048064 | tf_op jit(solution)/shard_map/ast,kt->ksa/dot_general | solution.py:167
  123.4 1.1 copy.140
  124.5 17.4 %exchange2.1 = bf16[8,32,1024]{2,1,0:T(8,128)(2,1)} custom-call(bf16[8,32,1024]{2,1,0:T(8,128)(2,1)} %bitcast.135), custom_call_target="tpu_custom_call" | custom-call | tf_op jit(solution)/shard_map/exchange2/pallas_call | solution.py:67
  141.9 1.9 copy.141
  143.8 11.5 %adjoint.3 = bf16[4,256,1024]{2,1,0:T(8,128)(2,1)} custom-call(bf16[256,1024]{1,0:T(8,128)(2,1)} %bitcast.122, bf16[2,1024,4096]{2,1,0:T(8,128)(2,1)} %bitcast.113), custom_call_target="tpu_custom_call" | custom-call | flops 4294967296 | bytes 19398656 | tf_op jit(solution)/shard_map/adjoint/pallas_call | solution.py:214
  155.3 1.3 dynamic-slice_bitcast_fusion
  156.7 0.1 collective-permute-start.4
  156.8 0.1 broadcast_multiply_fusion
  156.9 0.8 copy.135
  157.7 7.6 %all-to-all-start.2 = ((bf16[8,32,1024]{2,1,0:T(8,128)(2,1)}), bf16[8,32,1024]{2,1,0:T(8,128)(2,1)S(1)}, u32[]{:S(2)}, u32[]{:S(2)}) async-start(bf16[8,32,1024]{2,1,0:T(8,128)(2,1)} %bitcast.21), calls=%async_computation.2 | async-start | bytes 1048576 | tf_op jit(solution)/shard_map/all_to_all | solution.py:337
  165.3 2.0 fusion.12
  167.3 0.8 constant_dynamic-slice_fusion
  168.1 1.5 collective-permute-start.5
  169.6 0.2 copy.146.win_ref
  169.8 0.4 mul.127
  170.2 0.1 iota_compare_fusion.2
  170.3 10.1 %all-to-all-done.2 = bf16[8,32,1024]{2,1,0:T(8,128)(2,1)S(1)} async-done(((bf16[8,32,1024]{2,1,0:T(8,128)(2,1)}), bf16[8,32,1024]{2,1,0:T(8,128)(2,1)S(1)}, u32[]{:S(2)}, u32[]{:S(2)}) %all-to-all-start.2) | async-done | bytes 524320 | tf_op jit(solution)/shard_map/all_to_all | solution.py:337
  180.4 0.2 copy.144
  180.6 1.8 collective-permute-done.5
  182.5 1.2 add_convert_fusion
  183.7 0.8 copy.143
  184.5 14.0 %exchange3.1 = bf16[8,32,1024]{2,1,0:T(8,128)(2,1)} custom-call(bf16[8,32,1024]{2,1,0:T(8,128)(2,1)} %bitcast.137), custom_call_target="tpu_custom_call" | custom-call | tf_op jit(solution)/shard_map/exchange3/pallas_call | solution.py:67
  198.6 1.2 copy.145
  199.8 2.3 fusion.23
  202.1 2.2 multiply_reduce_fusion.1
  204.3 2.6 %pad_maximum_fusion.2 = f32[4]{0:T(128)S(1)} fusion(f32[1]{0:T(128)} %bitcast.56, f32[1]{0:T(128)} %bitcast.55, f32[1]{0:T(128)} %bitcast.41, f32[1]{0:T(128)} %bitcast.23), kind=kLoop, calls=%fused_computation.72 | loop fusion | flops 12 | bytes 32 | tf_op jit(solution)/shard_map/stack | solution.py:375
  206.9 0.1 broadcast_in_dim.7
  207.0 0.7 broadcast_in_dim.8.x_ref
  207.6 13.0 %total4.1.sums_ref = f32[8,128]{1,0:T(8,128)} custom-call(f32[8,128]{1,0:T(8,128)} %broadcast_in_dim.8.x_ref), custom_call_target="tpu_custom_call" | custom-call | tf_op jit(solution)/shard_map/total4/pallas_call | solution.py:114
  220.6 0.7 copy-done
  221.3 15.7 %final.1 = (f32[1024,16,128]{2,1,0:T(8,128)}, f32[1024,16,128]{2,1,0:T(8,128)}, f32[1024,16,128]{2,1,0:T(8,128)}) custom-call(f32[8,128]{1,0:T(8,128)S(1)} %copy-done, f32[1024,16,128]{2,1,0:T(8,128)} %rec_ref.1, f32[1024,32]{1,0:T(8,128)S(1)} %copy.146.win_ref, bf16[1024,256]{1,0:T(8,128)(2,1)S(1)} %bitcast.107, bf16[1024,256]{1,0:T(8,128)(2,1)S(1)} %bitcast.106, ...), custom_call_target="tpu_custom_call" | custom-call | flops 4294967296 | bytes 33554432 | tf_op jit(solution)/shard_map/final/pallas_call | solution.py:291
  (20 shorter events, 0.2 us)
Async XLA Ops:
  29.9 18.9 %copy-start.3 = (s32[8]{0:T(128)S(1)}, s32[8]{0:T(128)}, u32[]{:S(2)}) copy-start(s32[8]{0:T(128)} %param.9) | copy-start | bytes 100
  42.8 2.7 %collective-permute-start = (bf16[2,256,1024]{2,1,0:T(8,128)(2,1)S(1)}, bf16[2,256,1024]{2,1,0:T(8,128)(2,1)S(1)}, u32[]{:S(2)}, u32[]{:S(2)}) collective-permute-start(bf16[2,256,1024]{2,1,0:T(8,128)(2,1)S(1)} %dynamic-slice_bitcast_fusion.1), channel_id=1, source_target_pairs={{0,1},{1,0},{2,3},{3,2},{4,5},{5,4},{6,7},{7,6},{8,9},{9,8},{10,11... | collective-permute-start | bytes 3145736 | tf_op jit(solution)/shard_map/ppermute | solution.py:143
  47.2 14.0 %collective-permute-start.1 = (bf16[1,256,1024]{2,1,0:T(8,128)(2,1)S(1)}, bf16[1,256,1024]{2,1,0:T(8,128)(2,1)S(1)}, u32[]{:S(2)}, u32[]{:S(2)}) collective-permute-start(bf16[1,256,1024]{2,1,0:T(8,128)(2,1)S(1)} %constant_dynamic-slice_fusion.1), channel_id=1, source_target_pairs={{0,2},{1,3},{2,0},{3,1},{4,6},{5,7},{6,4},{7,5},{8,10},{9,11},{10,... | collective-permute-start | bytes 1572872 | tf_op jit(solution)/shard_map/ppermute | solution.py:143
  61.7 13.2 %collective-permute-start.2 = (bf16[256,1,1024]{2,0,1:T(8,128)(2,1)S(1)}, bf16[256,1,1024]{2,0,1:T(8,128)(2,1)S(1)}, u32[]{:S(2)}, u32[]{:S(2)}) collective-permute-start(bf16[256,1,1024]{2,0,1:T(8,128)(2,1)S(1)} %get-tuple-element.34), channel_id=1, source_target_pairs={{0,2},{1,3},{2,0},{3,1},{4,6},{5,7},{6,4},{7,5},{8,10},{9,11},{10,... | collective-permute-start | bytes 1572872 | tf_op jit(solution)/shard_map/ppermute | solution.py:156
  76.0 2.9 %collective-permute-start.3 = (bf16[256,2,1024]{2,0,1:T(8,128)(2,1)}, bf16[256,2,1024]{2,0,1:T(8,128)(2,1)S(1)}, u32[]{:S(2)}, u32[]{:S(2)}) collective-permute-start(bf16[256,2,1024]{2,0,1:T(8,128)(2,1)} %maximum_bitcast_fusion), channel_id=1, source_target_pairs={{0,1},{1,0},{2,3},{3,2},{4,5},{5,4},{6,7},{7,6},{8,9},{9,8},{10,11... | collective-permute-start | bytes 3145736 | tf_op jit(solution)/shard_map/ppermute | solution.py:156
  155.3 14.3 %copy-start.1 = (s32[1024,16]{0,1:T(8,128)S(1)}, s32[1024,16]{0,1:T(8,128)}, u32[]{:S(2)}) copy-start(s32[1024,16]{0,1:T(8,128)} %param.11) | copy-start | bytes 196612
  155.3 14.3 %copy-start.2 = (s32[1024,16]{0,1:T(8,128)S(1)}, s32[1024,16]{0,1:T(8,128)}, u32[]{:S(2)}) copy-start(s32[1024,16]{0,1:T(8,128)} %param.10) | copy-start | bytes 196612
  156.7 8.6 %collective-permute-start.4 = (bf16[2,256,1024]{2,1,0:T(8,128)(2,1)S(1)}, bf16[2,256,1024]{2,1,0:T(8,128)(2,1)}, u32[]{:S(2)}, u32[]{:S(2)}) collective-permute-start(bf16[2,256,1024]{2,1,0:T(8,128)(2,1)S(1)} %dynamic-slice_bitcast_fusion), channel_id=1, source_target_pairs={{0,1},{1,0},{2,3},{3,2},{4,5},{5,4},{6,7},{7,6},{8,9},{9,8},{10,11... | collective-permute-start | bytes 3145736 | tf_op jit(solution)/shard_map/ppermute | solution.py:143
  157.7 22.7 %all-to-all-start.2 = ((bf16[8,32,1024]{2,1,0:T(8,128)(2,1)}), bf16[8,32,1024]{2,1,0:T(8,128)(2,1)S(1)}, u32[]{:S(2)}, u32[]{:S(2)}) async-start(bf16[8,32,1024]{2,1,0:T(8,128)(2,1)} %bitcast.21), calls=%async_computation.2 | async-start | bytes 1048576 | tf_op jit(solution)/shard_map/all_to_all | solution.py:337
  168.1 14.4 %collective-permute-start.5 = (bf16[1,256,1024]{2,1,0:T(8,128)(2,1)}, bf16[1,256,1024]{2,1,0:T(8,128)(2,1)}, u32[]{:S(2)}, u32[]{:S(2)}) collective-permute-start(bf16[1,256,1024]{2,1,0:T(8,128)(2,1)} %constant_dynamic-slice_fusion), channel_id=1, source_target_pairs={{0,2},{1,3},{2,0},{3,1},{4,6},{5,7},{6,4},{7,5},{8,10},{9,11},{10,... | collective-permute-start | bytes 1572872 | tf_op jit(solution)/shard_map/ppermute | solution.py:143
  220.6 0.7 copy-start
where the time goes:
time: 239 us; the launch traced here: 237 us
  Pallas kernels  117 us (49%)
  waiting for transfers between devices  40 us (17%)
  matrix products  33.4 us (14%)
  local copies, waits for them, and re-layouts  18.4 us (8%)
  other arithmetic  13.6 us (6%)
  starting transfers between devices  12.4 us (5%)
    pallas_call x4, Pallas kernels, exchange(): pl.pallas_call(functools.partial(exchange_kernel, n), out_shape=jax.Shape...  65.6 us
    pallas_call x2, Pallas kernels, adjoint_product(): pl.pallas_call(adjoint_kernel, grid=(columns // tile,), out_shape=jax.Sha...  23.1 us
    pallas_call x1, Pallas kernels, final_step(): pl.pallas_call(final_kernel, grid=(points // tile,), out_shape=[jax.Shape...  15.7 us
    ppermute x4, waiting for transfers between devices, scatter_sum(): got = lax.ppermute(send, 'ma', pairs(n, bit))  15.4 us
    dot_general x2, matrix products, to_spectra(): jnp.einsum('ast,kt->ksa', traces.astype(jnp.bfloat16), flat, preferred_el...  14.9 us
    ppermute x2, waiting for transfers between devices, gather_all(): got = lax.ppermute(held, 'ma', pairs(n, bit))  14.4 us
    pallas_call x1, Pallas kernels, total(): pl.pallas_call(functools.partial(total_kernel, outer, inner), out_shape=j...  13 us
    all_to_all x1, waiting for transfers between devices, per_device(): lax.all_to_all(by_source(adjoint, outer), 'gx', split_axis=0, concat_axis...  10.1 us
  transfers between devices with their start and end apart: 7, of which 6 were waited for; matrix products, arithmetic and copies ran while one was open for 2% of the time, Pallas kernels for 0%

commit v1 on v0

--- a/solution.py
+++ b/solution.py
@@ -326,7 +326,670 @@
     return jnp.stack([real_part, imaginary], 0).astype(jnp.bfloat16)
 
 
+RECORDED, RETURNED, IMAGED, SECOND, CHANGED, MIXED = range(6)
+
+
+def iteration_kernel(
+    outer, inner, mixing, rec_ref, ker_ref, win_ref, tall_ref, across_ref, same_ref,
+    returned_ref, imaged_ref, changed_ref, sums_ref,
+    traces, gains, window, spread, gather, tapered, first_out, first_in, second_out, second_in,
+    total, product, image_out, core_out, core_in, line_out, line_in, model, summed, normal,
+    mixed_out, stats, stats_in, stats_all,
+    trace_sem, gain_sem, out_sem, in_sem, core_out_sem, core_in_sem, line_out_sem, line_in_sem,
+    share_out_sem, share_in_sem, stats_out_sem, stats_in_sem,
+):
+    n = outer
+    sources, points, length = traces.shape
+    chunks, _, double, width = first_out.shape
+    pieces, piece = model.shape[1], model.shape[4]
+    depth = n * double
+    block = pieces * piece
+    f32, bf16 = jnp.float32, jnp.bfloat16
+    me, mine = lax.axis_index("gx"), lax.axis_index("ma")
+    core = mine + 1 - 2 * lax.rem(mine, 2)
+    line = lax.rem(mine + 2, 4)
+    corner = lax.rem(core + 2, 4)
+
+    def loop(start, stop, body):
+        def step(i, carry):
+            body(i)
+            return carry
+
+        lax.fori_loop(start, stop, step, 0)
+
+    def part(i):
+        return pl.ds(pl.multiple_of(i * width, width), width)
+
+    def trace_copy(i, s):
+        return pltpu.make_async_copy(
+            rec_ref.at[part(i), s], traces.at[s, part(i)], trace_sem.at[i, s]
+        )
+
+    def gain_copy(i):
+        return pltpu.make_async_copy(
+            ker_ref.at[:, part(i)], gains.at[:, part(i)], gain_sem.at[i]
+        )
+
+    def across(number, src, dst, i, k, peer, slot):
+        return pltpu.make_async_remote_copy(
+            src_ref=src.at[i, peer],
+            dst_ref=dst.at[i, slot],
+            send_sem=out_sem.at[number, i, k],
+            recv_sem=in_sem.at[number, i, k],
+            device_id={"gx": peer},
+            device_id_type=MESH,
+        )
+
+    def send_all(number, src, dst, i):
+        def body(k):
+            peer = lax.rem(me + k, n)
+            across(number, src, dst, i, k, peer, me).start()
+
+        loop(1, n, body)
+        dst[i, me] = src[i, me]
+
+    def receive_all(number, src, dst, i):
+        def body(k):
+            peer = lax.rem(me + n - k, n)
+            across(number, src, dst, i, k, peer, peer).wait_recv()
+
+        loop(1, n, body)
+
+    def finish_all(number, src, dst, count):
+        def outside(i):
+            def body(k):
+                peer = lax.rem(me + k, n)
+                across(number, src, dst, i, k, peer, me).wait_send()
+
+            loop(1, n, body)
+
+        loop(0, count, outside)
+
+    def core_copy(stage, which, p):
+        return pltpu.make_async_remote_copy(
+            src_ref=core_out.at[stage, which, p],
+            dst_ref=core_in.at[stage, which, p],
+            send_sem=core_out_sem.at[stage, which, p],
+            recv_sem=core_in_sem.at[stage, which, p],
+            device_id={"ma": core},
+            device_id_type=MESH,
+        )
+
+    def line_copy(stage, p):
+        return pltpu.make_async_remote_copy(
+            src_ref=line_out.at[stage, p],
+            dst_ref=line_in.at[stage, p],
+            send_sem=line_out_sem.at[stage, p],
+            recv_sem=line_in_sem.at[stage, p],
+            device_id={"ma": line},
+            device_id_type=MESH,
+        )
+
+    def share_copy(which, p):
+        source, slot, peer = ((0, 1, core), (0, 2, line), (2, 3, core))[which]
+        return pltpu.make_async_remote_copy(
+            src_ref=model.at[source, p],
+            dst_ref=model.at[slot, p],
+            send_sem=share_out_sem.at[which, p],
+            recv_sem=share_in_sem.at[which, p],
+            device_id={"ma": peer},
+            device_id_type=MESH,
+        )
+
+    barrier = pltpu.get_barrier_semaphore()
+
+    def greet(k):
+        pl.semaphore_signal(
+            barrier, inc=1, device_id={"gx": lax.rem(me + k, n)}, device_id_type=MESH
+        )
+
+    loop(1, n, greet)
+    for peer in (core, line):
+        pl.semaphore_signal(barrier, inc=1, device_id={"ma": peer}, device_id_type=MESH)
+
+    def load(i):
+        loop(0, sources, lambda s: trace_copy(i, s).start())
+
+    loop(0, chunks, load)
+    for s in range(sources):
+        rows = lax.broadcasted_iota(jnp.int32, (depth, length), 0)
+        spread[:, s * length : (s + 1) * length] = jnp.where(
+            lax.rem(rows, sources) == s, tall_ref[...], 0.0
+        ).astype(bf16)
+        columns = lax.broadcasted_iota(jnp.int32, (length, depth), 1)
+        gather[s * length : (s + 1) * length] = jnp.where(
+            lax.rem(columns, sources) == s, across_ref[...], 0.0
+        ).astype(bf16)
+    stats[...] = jnp.zeros_like(stats)
+    pl.semaphore_wait(barrier, n + 1)
+
+    samples = lax.broadcasted_iota(jnp.int32, (length, width), 0).astype(f32) * (1.0 / RAMP)
+
+    def span(s):
+        return pl.ds(pl.multiple_of(s * length, length), length)
+
+    def transform(out, i):
+        result = jnp.dot(spread[...], tapered[...], preferred_element_type=f32)
+        out[i] = result.astype(bf16).reshape(n, double, width)
+
+    def record(i):
+        loop(0, sources, lambda s: trace_copy(i, s).wait())
+        gain_copy(i).start()
+
+        def taper(s):
+            rising = jnp.clip(samples + win_ref[pl.ds(s, 1), part(i)], 0.0, 1.0)
+            falling = jnp.clip(win_ref[pl.ds(sources + s, 1), part(i)] - samples, 0.0, 1.0)
+            weight = rising * falling
+            window[i, span(s)] = weight.astype(bf16)
+            tapered[span(s)] = (weight * traces[s, part(i)].T).astype(bf16)
+
+        loop(0, sources, taper)
+        transform(first_out, i)
+        send_all(RECORDED, first_out, first_in, i)
+
+    loop(0, chunks, record)
+
+    def turned(values, sign):
+        half = double // 2
+        low, high = values[:, :half], values[:, half:]
+        pair = [high, -low] if sign > 0 else [-high, low]
+        return jnp.concatenate(pair, 1).reshape(depth, values.shape[2])
+
+    def adjoint_part(held, i, columns):
+        data = held[i]
+        return jnp.dot(
+            data.reshape(depth, width), gains[0, part(i), columns], preferred_element_type=f32
+        ) + jnp.dot(turned(data, 1), gains[1, part(i), columns], preferred_element_type=f32)
+
+    def accumulate(held, i, first):
+        def body(j):
+            columns = pl.ds(pl.multiple_of(j * block, block), block)
+            update = adjoint_part(held, i, columns)
+            total[:, columns] = update if first else total[:, columns] + update
+
+        loop(0, inner, body)
+
+    def adjoint(number, src, held, stage, use):
+        for i in range(chunks - 1):
+            receive_all(number, src, held, i)
+            if stage == 0:
+                gain_copy(i).wait()
+            accumulate(held, i, i == 0)
+        last = chunks - 1
+        receive_all(number, src, held, last)
+        if stage == 0:
+            gain_copy(last).wait()
+
+        def tile(where, p):
+            columns = pl.ds(pl.multiple_of(where * block + p * piece, piece), piece)
+            update = adjoint_part(held, last, columns)
+            return update if chunks == 1 else total[:, columns] + update
+
+        def pack(values):
+            return values.astype(bf16).reshape(n, double, piece)
+
+        def to_core(which, where):
+            def body(p):
+                core_out[stage, which, p] = pack(tile(where, p))
+                core_copy(stage, which, p).start()
+
+            loop(0, pieces, body)
+
+        def from_core(which, p):
+            core_copy(stage, which, p).wait_recv()
+            return core_in[stage, which, p].reshape(depth, piece).astype(f32)
+
+        def to_line(p):
+            values = tile(line, p)
+            line_out[stage, p] = pack(values + from_core(0, p))
+            line_copy(stage, p).start()
+
+        def own(p):
+            values = tile(mine, p)
+            values = values + from_core(1, p)
+            line_copy(stage, p).wait_recv()
+            values = values + line_in[stage, p].reshape(depth, piece).astype(f32)
+            use(p, pack(values))
+
+        to_core(0, corner)
+        loop(0, pieces, to_line)
+        to_core(1, core)
+        loop(0, pieces, own)
+
+    def folded(values):
+        rows, columns = values.shape
+        parts = values.reshape(rows // 8, 8, columns).sum(0)
+        out = parts[:, :128]
+        for j in range(1, columns // 128):
+            out = out + parts[:, j * 128 : (j + 1) * 128]
+        return out
+
+    def flat(values):
+        return values.reshape(depth, values.shape[2]).astype(f32)
+
+    def forward_part(slot, where, p, rows):
+        columns = pl.ds(pl.multiple_of(where * block + p * piece, piece), piece)
+        values = model[slot, p]
+        dims = (((1,), (1,)), ((), ()))
+        return lax.dot_general(
+            gains[0, rows, columns],
+            values.reshape(depth, piece),
+            dims,
+            preferred_element_type=f32,
+        ) + lax.dot_general(
+            gains[1, rows, columns], turned(values, -1), dims, preferred_element_type=f32
+        )
+
+    def forward(slot, where, p, first=False):
+        tile_rows = 2 * width if chunks % 2 == 0 else width
+
+        def body(i):
+            rows = pl.ds(pl.multiple_of(i * tile_rows, tile_rows), tile_rows)
+            update = forward_part(slot, where, p, rows)
+            product[rows] = update if first else product[rows] + update
+
+        loop(0, points // tile_rows, body)
+
+    def share(p):
+        share_copy(1, p).start()
+        share_copy(0, p).start()
+
+    if mixing:
+
+        def keep(p, values):
+            summed[p] = values
+            send_all(RETURNED, summed, returned_ref, p)
+
+        adjoint(RECORDED, first_out, first_in, 0, keep)
+
+        def mix(p):
+            receive_all(RETURNED, summed, returned_ref, p)
+            arrived = returned_ref[p].reshape(depth, piece)
+            values = jnp.dot(same_ref[...], arrived, preferred_element_type=f32)
+            mixed_out[p] = values.astype(bf16).reshape(n, double, piece)
+            send_all(MIXED, mixed_out, model.at[0], p)
+
+        loop(0, pieces, mix)
+
+        def spread_out(p):
+            receive_all(MIXED, mixed_out, model.at[0], p)
+            share(p)
+
+        loop(0, pieces, spread_out)
+    else:
+
+        def keep(p, values):
+            model[0, p] = values
+            share(p)
+            send_all(RETURNED, model.at[0], returned_ref, p)
+            held = flat(values)
+            stats[0] += folded(held * held)
+
+        adjoint(RECORDED, first_out, first_in, 0, keep)
+
+    product[...] = jnp.zeros_like(product)
+    loop(0, pieces, lambda p: forward(0, mine, p))
+
+    def from_share(p):
+        share_copy(0, p).wait_recv()
+        forward(1, core, p)
+
+    loop(0, pieces, from_share)
+
+    def relay(p):
+        share_copy(1, p).wait_recv()
+        share_copy(2, p).start()
+
+    def from_line(p):
+        relay(p)
+        forward(2, line, p)
+        share_copy(2, p).wait_recv()
+        forward(3, corner, p)
+
+    loop(0, pieces - 1, from_line)
+    final = pieces - 1
+    relay(final)
+    forward(2, line, final)
+    share_copy(2, final).wait_recv()
+
+    def imaging(i):
+        values = product[part(i)] + forward_part(3, corner, final, part(i))
+        image_out[i] = values.T.astype(bf16).reshape(n, double, width)
+        send_all(IMAGED, image_out, imaged_ref, i)
+
+    loop(0, chunks, imaging)
+
+    def again(i):
+        receive_all(IMAGED, image_out, imaged_ref, i)
+        arrived = imaged_ref[i].reshape(depth, width)
+
+        def taper(s):
+            weight = window[i, span(s)].astype(f32)
+            values = jnp.dot(gather[span(s)], arrived, preferred_element_type=f32) * weight
+            stats[1] += folded(values * values)
+            tapered[span(s)] = (values * weight).astype(bf16)
+
+        loop(0, sources, taper)
+        transform(second_out, i)
+        send_all(SECOND, second_out, second_in, i)
+
+    loop(0, chunks, again)
+
+    def change(p, values):
+        normal[p] = values
+        send_all(CHANGED, normal, changed_ref, p)
+        if not mixing:
+            held = flat(values)
+            stats[2] += folded(held * flat(model[0, p]))
+            stats[3] += folded(held * held)
+
+    adjoint(SECOND, second_out, second_in, 1, change)
+    if mixing:
+
+        def norms(p):
+            receive_all(CHANGED, normal, changed_ref, p)
+            before = returned_ref[p].reshape(depth, piece)
+            after = changed_ref[p].reshape(depth, piece)
+            mixed_before = jnp.dot(same_ref[...], before, preferred_element_type=f32)
+            mixed_after = jnp.dot(same_ref[...], after, preferred_element_type=f32)
+            stats[0] += folded(before.astype(f32) * mixed_before)
+            stats[2] += folded(after.astype(f32) * mixed_before)
+            stats[3] += folded(after.astype(f32) * mixed_after)
+
+        loop(0, pieces, norms)
+
+    def stats_copy(which, src, peer):
+        return pltpu.make_async_remote_copy(
+            src_ref=src,
+            dst_ref=stats_in.at[which],
+            send_sem=stats_out_sem.at[which],
+            recv_sem=stats_in_sem.at[which],
+            device_id={"ma": peer},
+            device_id_type=MESH,
+        )
+
+    def stats_across(k, peer, slot):
+        return pltpu.make_async_remote_copy(
+            src_ref=stats_in.at[3],
+            dst_ref=stats_all.at[slot],
+            send_sem=stats_out_sem.at[2 + k],
+            recv_sem=stats_in_sem.at[2 + k],
+            device_id={"gx": peer},
+            device_id_type=MESH,
+        )
+
+    to_core = stats_copy(0, stats, core)
+    to_core.start()
+    to_core.wait_recv()
+    stats_in[2] = stats[...] + stats_in[0]
+    to_line = stats_copy(1, stats_in.at[2], line)
+    to_line.start()
+    to_line.wait_recv()
+    stats_in[3] = stats_in[2] + stats_in[1]
+    loop(1, n, lambda k: stats_across(k, lax.rem(me + k, n), me).start())
+    stats_all[me] = stats_in[3]
+
+    def stats_wait(k):
+        peer = lax.rem(me + n - k, n)
+        stats_across(k, peer, peer).wait_recv()
+
+    loop(1, n, stats_wait)
+    sums_ref[...] = jnp.sum(stats_all[...], axis=0)
+    if not mixing:
+        loop(0, pieces, lambda p: receive_all(RETURNED, model.at[0], returned_ref, p))
+        loop(0, pieces, lambda p: receive_all(CHANGED, normal, changed_ref, p))
+
+    to_core.wait_send()
+    to_line.wait_send()
+    loop(1, n, lambda k: stats_across(k, lax.rem(me + k, n), me).wait_send())
+    finish_all(RECORDED, first_out, first_in, chunks)
+    finish_all(RETURNED, summed if mixing else model.at[0], returned_ref, pieces)
+    finish_all(IMAGED, image_out, imaged_ref, chunks)
+    finish_all(SECOND, second_out, second_in, chunks)
+    finish_all(CHANGED, normal, changed_ref, pieces)
+    if mixing:
+        finish_all(MIXED, mixed_out, model.at[0], pieces)
+
+    def finish(p):
+        for stage in range(2):
+            core_copy(stage, 0, p).wait_send()
+            core_copy(stage, 1, p).wait_send()
+            line_copy(stage, p).wait_send()
+        for which in range(3):
+            share_copy(which, p).wait_send()
+
+    loop(0, pieces, finish)
+
+
+def iteration(outer, inner, mixing, recorded, kernel, windows, tall, across, same):
+    points, sources, length = recorded.shape
+    columns = kernel.shape[2]
+    double = 2 * sources
+    depth = outer * double
+    block = columns // inner
+    width, piece = min(256, points), min(256, block)
+    chunks, pieces = points // width, block // piece
+    f32, bf16 = jnp.float32, jnp.bfloat16
+    by_chunk = (chunks, outer, double, width)
+    by_piece = (pieces, outer, double, piece)
+    vmem = pl.BlockSpec(memory_space=pltpu.VMEM)
+    hbm = pl.BlockSpec(memory_space=pl.ANY)
+    dma = pltpu.SemaphoreType.DMA
+    exchanges = 6 if mixing else 5
+    most = max(chunks, pieces)
+    extra = by_piece if mixing else (1, 1, 16, 128)
+    return pl.pallas_call(
+        functools.partial(iteration_kernel, outer, inner, mixing),
+        out_shape=[
+            jax.ShapeDtypeStruct(by_piece, bf16),
+            jax.ShapeDtypeStruct(by_chunk, bf16),
+            jax.ShapeDtypeStruct(by_piece, bf16),
+            jax.ShapeDtypeStruct((4, 8, 128), f32),
+        ],
+        in_specs=[hbm, hbm, vmem, vmem, vmem, vmem],
+        out_specs=[vmem] * 4,
+        scratch_shapes=[
+            pltpu.VMEM((sources, points, length), f32),
+            pltpu.VMEM((2, points, columns), bf16),
+            pltpu.VMEM((chunks, sources * length, width), bf16),
+            pltpu.VMEM((depth, sources * length), bf16),
+            pltpu.VMEM((sources * length, depth), bf16),
+            pltpu.VMEM((sources * length, width), bf16),
+            pltpu.VMEM(by_chunk, bf16),
+            pltpu.VMEM(by_chunk, bf16),
+            pltpu.VMEM(by_chunk, bf16),
+            pltpu.VMEM(by_chunk, bf16),
+            pltpu.VMEM((depth, columns), f32),
+            pltpu.VMEM((points, depth), f32),
+            pltpu.VMEM(by_chunk, bf16),
+            pltpu.VMEM((2, 2) + by_piece, bf16),
+            pltpu.VMEM((2, 2) + by_piece, bf16),
+            pltpu.VMEM((2,) + by_piece, bf16),
+            pltpu.VMEM((2,) + by_piece, bf16),
+            pltpu.VMEM((4,) + by_piece, bf16),
+            pltpu.VMEM(extra, bf16),
+            pltpu.VMEM(by_piece, bf16),
+            pltpu.VMEM(extra, bf16),
+            pltpu.VMEM((4, 8, 128), f32),
+            pltpu.VMEM((4, 4, 8, 128), f32),
+            pltpu.VMEM((outer, 4, 8, 128), f32),
+            dma((chunks, sources)),
+            dma((chunks,)),
+            dma((exchanges, most, outer)),
+            dma((exchanges, most, outer)),
+            dma((2, 2, pieces)),
+            dma((2, 2, pieces)),
+            dma((2, pieces)),
+            dma((2, pieces)),
+            dma((3, pieces)),
+            dma((3, pieces)),
+            dma((2 + outer,)),
+            dma((2 + outer,)),
+        ],
+        compiler_params=pltpu.CompilerParams(
+            collective_id=6 if mixing else 5,
+            has_side_effects=True,
+            vmem_limit_bytes=67_000_000,
+        ),
+        name="iteration_mixed" if mixing else "iteration",
+    )(recorded, kernel, windows, tall, across, same)
+
+
+def write_kernel(
+    sums_ref, rec_ref, win_ref, tall_ref, across_ref, ret_ref, ima_ref, cha_ref,
+    sol_ref, res_ref, dir_ref,
+    traces, spread, gather, solved, rest, ahead, in_sem, out_sem,
+):
+    sources, points, length = traces.shape
+    chunks, outer, double, width = ima_ref.shape
+    depth = outer * double
+    f32, bf16 = jnp.float32, jnp.bfloat16
+
+    def loop(start, stop, body):
+        def step(i, carry):
+            body(i)
+            return carry
+
+        lax.fori_loop(start, stop, step, 0)
+
+    def part(i):
+        return pl.ds(pl.multiple_of(i * width, width), width)
+
+    def load(i, s):
+        return pltpu.make_async_copy(
+            rec_ref.at[part(i), s], traces.at[s, part(i)], in_sem.at[i, s]
+        )
+
+    def store(number, i, s):
+        src, dst = ((solved, sol_ref), (ahead, dir_ref), (rest, res_ref))[number]
+        return pltpu.make_async_copy(
+            src.at[s, part(i)], dst.at[part(i), s], out_sem.at[number, i, s]
+        )
+
+    loop(0, chunks, lambda i: loop(0, sources, lambda s: load(i, s).start()))
+    for s in range(sources):
+        rows = lax.broadcasted_iota(jnp.int32, (depth, length), 0)
+        spread[s] = jnp.where(lax.rem(rows, sources) == s, tall_ref[...], 0.0).astype(bf16)
+        columns = lax.broadcasted_iota(jnp.int32, (length, depth), 1)
+        gather[s] = jnp.where(lax.rem(columns, sources) == s, across_ref[...], 0.0).astype(bf16)
+    norm_start, norm_data = jnp.sum(sums_ref[0]), jnp.sum(sums_ref[1])
+    cross, norm_change = jnp.sum(sums_ref[2]), jnp.sum(sums_ref[3])
+    step_size = norm_start / (norm_data + epsilon)
+    norm_final = norm_start - 2.0 * step_size * cross + step_size * step_size * norm_change
+    ratio = norm_final / (norm_start + epsilon)
+    samples = lax.broadcasted_iota(jnp.int32, (length, width), 0).astype(f32) * (1.0 / RAMP)
+
+    def chunk(i):
+        before = ret_ref[i].reshape(depth, width).astype(f32).T.astype(bf16)
+        after = cha_ref[i].reshape(depth, width).astype(f32).T.astype(bf16)
+        arrived = ima_ref[i].reshape(depth, width)
+
+        def one(s):
+            gradient = jnp.dot(before, spread[s], preferred_element_type=f32)
+            change = jnp.dot(after, spread[s], preferred_element_type=f32)
+            solved[s, part(i)] = step_size * gradient
+            ahead[s, part(i)] = (gradient - step_size * change) + ratio * gradient
+            store(0, i, s).start()
+            store(1, i, s).start()
+            rising = jnp.clip(samples + win_ref[pl.ds(s, 1), part(i)], 0.0, 1.0)
+            falling = jnp.clip(win_ref[pl.ds(sources + s, 1), part(i)] - samples, 0.0, 1.0)
+            image = jnp.dot(gather[s], arrived, preferred_element_type=f32)
+            image = (rising * falling) * image
+            load(i, s).wait()
+            rest[s, part(i)] = traces[s, part(i)] - step_size * image.T
+            store(2, i, s).start()
+
+        loop(0, sources, one)
+
+    loop(0, chunks, chunk)
+
+    def finish(i):
+        def one(s):
+            for number in range(3):
+                store(number, i, s).wait()
+
+        loop(0, sources, one)
+
+    loop(0, chunks, finish)
+
+
+def write(sums, recorded, windows, tall, across, returned, imaged, changed):
+    points, sources, length = recorded.shape
+    chunks, outer, double, width = imaged.shape
+    depth = outer * double
+    vmem = pl.BlockSpec(memory_space=pltpu.VMEM)
+    hbm = pl.BlockSpec(memory_space=pl.ANY)
+    f32, bf16 = jnp.float32, jnp.bfloat16
+    staged = pltpu.VMEM((sources, points, length), f32)
+    return pl.pallas_call(
+        write_kernel,
+        out_shape=[jax.ShapeDtypeStruct(recorded.shape, f32)] * 3,
+        in_specs=[vmem, hbm] + [vmem] * 6,
+        out_specs=[hbm] * 3,
+        scratch_shapes=[
+            staged,
+            pltpu.VMEM((sources, depth, length), bf16),
+            pltpu.VMEM((sources, length, depth), bf16),
+            staged,
+            staged,
+            staged,
+            pltpu.SemaphoreType.DMA((chunks, sources)),
+            pltpu.SemaphoreType.DMA((3, chunks, sources)),
+        ],
+        compiler_params=pltpu.CompilerParams(vmem_limit_bytes=56 * 1024 * 1024),
+        cost_estimate=pl.CostEstimate(
+            flops=6 * points * sources * depth * length,
+            bytes_accessed=16 * points * sources * length,
+            transcendentals=0,
+        ),
+        name="write",
+    )(sums, recorded, windows, tall, across, returned, imaged, changed)
+
+
+def fused(outer, inner, recorded, kernel, freq_bins, window_start, window_stop):
+    points, sources, length = recorded.shape
+    double = 2 * sources
+    depth = outer * double
+    table = phase_table(freq_bins, length).astype(jnp.bfloat16).astype(jnp.float32)
+    tall = jnp.repeat(table.reshape(-1, length), sources, axis=0)
+    windows = jnp.concatenate(
+        [(1 - window_start).astype(jnp.float32) / RAMP, window_stop.astype(jnp.float32) / RAMP], 1
+    ).T
+    same = freq_bins[:, None] == freq_bins[None, :]
+    repeated = jnp.sum(same.astype(jnp.int32)) > freq_bins.shape[0]
+    eye = jnp.eye(double, dtype=jnp.bfloat16)
+    mixing = (same.astype(jnp.bfloat16)[:, None, :, None] * eye[None, :, None, :]).reshape(
+        depth, depth
+    )
+    gains = kernel.reshape(2, kernel.shape[2], kernel.shape[3])
+    operands = (recorded, gains, windows, tall, tall.T, mixing)
+    returned, imaged, changed, sums = lax.cond(
+        repeated,
+        lambda *x: tuple(iteration(outer, inner, True, *x)),
+        lambda *x: tuple(iteration(outer, inner, False, *x)),
+        *operands,
+    )
+    return tuple(write(sums, recorded, windows, tall, tall.T, returned, imaged, changed))
+
+
+def fits(outer, inner, recorded, kernel):
+    points, sources, length = recorded.shape
+    columns = kernel.shape[3]
+    return (
+        inner == 4
+        and kernel.shape[1] == 1
+        and columns == inner * points
+        and sources % 16 == 0
+        and length % 128 == 0
+        and points % 256 == 0
+        and (outer * 2 * sources) % 128 == 0
+        and points * (4 * columns + 6 * sources * length) < 30_000_000
+    )
+
+
 def per_device(outer, inner, recorded, kernel, freq_bins, window_start, window_stop):
+    if fits(outer, inner, recorded, kernel):
+        return fused(outer, inner, recorded, kernel, freq_bins, window_start, window_stop)
     length = recorded.shape[2]
     table = phase_table(freq_bins, length)
     weights = taper_weights(window_start, window_stop, length)

time: 239 us -> 145 us (0.61)
  waiting for transfers between devices: 40 us -> 0 us
  matrix products: 33.4 us -> 0 us
  Pallas kernels: 117 us -> 135 us
  local copies, waits for them, and re-layouts: 18.4 us -> 3.35 us
  starting transfers between devices: 12.4 us -> 0 us
  other arithmetic: 13.6 us -> 4.67 us
    dot_general x6 -> x0, matrix products: 33.4 us -> none  [the longest x2 14.9 us: to_spectra(): jnp.einsum('ast,kt->ksa', traces.astype(jnp.bfloat16), flat, preferred_el...]
    ppermute x6 -> x0, waiting for transfers between devices: 29.9 us -> none  [the longest x4 15.4 us: scatter_sum(): got = lax.ppermute(send, 'ma', pairs(n, bit))]
    pallas_call x8 -> x2, Pallas kernels: 117 us -> 135 us  [the longest x1 107 us: iteration(): pl.pallas_call(functools.partial(iteration_kernel, outer, inner, mixing),...]
    all_to_all x1 -> x0, waiting for transfers between devices: 10.1 us -> none  [per_device(): lax.all_to_all(by_source(adjoint, outer), 'gx', split_axis=0, concat_axis...]
    all_to_all x1 -> x0, starting transfers between devices: 7.57 us -> none  [per_device(): lax.all_to_all(by_source(adjoint, outer), 'gx', split_axis=0, concat_axis...]
    convert_element_type x11 -> x3, other arithmetic: 6.75 us -> 0.82 us  [the longest x1 0.8 us: fused(): same.astype(jnp.bfloat16)[:, None, :, None] * eye[None, :, None, :]]
    ppermute x6 -> x0, starting transfers between devices: 4.83 us -> none  [the longest x4 3.24 us: scatter_sum(): got = lax.ppermute(send, 'ma', pairs(n, bit))]
    reshape x5 -> x1, local copies, waits for them, and re-layouts: 6.45 us -> 1.65 us  [fused(): tall = jnp.repeat(table.reshape(-1, length), sources, axis=0)]
  transfers between devices with their start and end apart: 7 -> 0, of which waited for: 6 -> 0; matrix products, arithmetic and copies ran while one was open for 2% -> 0% of each run, Pallas kernels for 0% -> 0%
where the time goes in v1:
time: 145 us
  Pallas kernels  135 us (93%)
  other arithmetic  4.67 us (3%)
  local copies, waits for them, and re-layouts  3.35 us (2%)
  between operations  1.48 us (1%)
    pallas_call x1, Pallas kernels, iteration(): pl.pallas_call(functools.partial(iteration_kernel, outer, inner, mixing),...  107 us
    pallas_call x1, Pallas kernels, write(): pl.pallas_call(write_kernel, out_shape=[jax.ShapeDtypeStruct(recorded.sha...  27.8 us

profile of v1, /device:TPU:0, one launch (start us, length us, event | category | flops | bytes accessed | tf_op | source)
XLA Modules:
  0.0 144.6 jit_solution(15500540723304446685)
XLA Ops:
  0.6 1.4 fusion.2
  2.7 0.8 compare_convert_fusion
  3.5 0.8 fusion.10
  4.3 0.7 broadcast_in_dim.2
  5.0 1.7 %copy.13 = f32[256,128]{0,1:T(8,128)} copy(f32[256,128]{1,0:T(8,128)} %bitcast.3.tall_ref) | data formatting | bytes 262144 | tf_op jit(solution)/shard_map/reshape | solution.py:954
  6.7 0.9 convert_multiply_fusion
  7.5 0.7 maximum_bitcast_fusion.win_ref
  8.2 0.1 broadcast_multiply_fusion
  8.3 1.0 mul.76
  9.3 107.3 %conditional.1 = ((bf16[4,8,32,256]{3,2,1,0:T(8,128)(2,1)}, bf16[4,8,32,256]{3,2,1,0:T(8,128)(2,1)}, bf16[4,8,32,256]{3,2,1,0:T(8,128)(2,1)}, f32[4,8,128]{2,1,0:T(8,128)S(1)})) conditional(s32[]{:T(128)} %convert_element_type.53, (f32[1024,16,128]{2,1,0:T(8,128)}, bf16[2,1024,4096]{2,1,0:T(8,128)(2,1)}, f32[32,1024]{1,0:T(8,128)}, ...), branch_computations={%region_1.2_spmd, %region_2.3_spmd} | conditional | bytes 8 | solution.py:966
  9.3 107.1 %iteration.1 = (bf16[4,8,32,256]{3,2,1,0:T(8,128)(2,1)}, bf16[4,8,32,256]{3,2,1,0:T(8,128)(2,1)}, bf16[4,8,32,256]{3,2,1,0:T(8,128)(2,1)}, f32[4,8,128]{2,1,0:T(8,128)S(1)}) custom-call(f32[1024,16,128]{2,1,0:T(8,128)} %get-tuple-element.24.rec_ref, bf16[2,1024,4096]{2,1,0:T(8,128)(2,1)} %get-tuple-element.25.ker_ref, f32[32,1024]{1,0:T(8,128)} %get-tuple-element.26.win_ref, ...), custom_call_target="tpu_custom_call" | custom-call | tf_op jit(solution)/shard_map/cond/branch_0_fun/iteration/pallas_call | solution.py:781
  116.6 27.8 %write.1 = (f32[1024,16,128]{2,1,0:T(8,128)}, f32[1024,16,128]{2,1,0:T(8,128)}, f32[1024,16,128]{2,1,0:T(8,128)}) custom-call(f32[4,8,128]{2,1,0:T(8,128)S(1)} %get-tuple-element.43.sums_ref, f32[1024,16,128]{2,1,0:T(8,128)} %rec_ref.1, f32[32,1024]{1,0:T(8,128)} %maximum_bitcast_fusion.win_ref, f32[256,128]{1,0:T(8,128)} %bitcast.3.tall_ref, ...), custom_call_target="tpu_custom_call" | custom-call | flops 3221225472 | bytes 33554432 | tf_op jit(solution)/shard_map/write/pallas_call | solution.py:924
  (3 shorter events, 0.0 us)

commit v2 on v0

--- a/solution.py
+++ b/solution.py
@@ -326,7 +326,770 @@
     return jnp.stack([real_part, imaginary], 0).astype(jnp.bfloat16)
 
 
+RECORDED, RETURNED, IMAGED, SECOND, CHANGED, MIXED = range(6)
+PARTS = 2
+GROUP = 4
+
+
+def loop(start, stop, body):
+    def step(i, carry):
+        body(i)
+        return carry
+
+    lax.fori_loop(start, stop, step, 0)
+
+
+def iota(shape, axis):
+    return lax.broadcasted_iota(jnp.int32, shape, axis)
+
+
+def folded(values):
+    rows, columns = values.shape
+    parts = values.reshape(rows // 8, 8, columns).sum(0)
+    out = parts[:, :128]
+    for j in range(1, columns // 128):
+        out = out + parts[:, j * 128 : (j + 1) * 128]
+    return out
+
+
+def iteration_kernel(
+    outer, inner, mixing, bins_ref, rec_ref, ker_ref, start_ref, stop_ref,
+    returned_ref, imaged_ref, changed_ref, sums_ref, win_ref, spread_ref, gather_ref,
+    traces, gains, window, win, spread, gather, tapered, first_out, first_in, second_out,
+    second_in, total, product, image_out, image_in, core_out, core_in, line_out, line_in, model,
+    summed, summed_in, normal, normal_in, mixed_out, same, stats, stats_in, stats_all,
+    trace_sem, gain_sem, keep_sem, out_sem, in_sem, core_out_sem, core_in_sem, line_out_sem,
+    line_in_sem, share_out_sem, share_in_sem, stats_out_sem, stats_in_sem,
+):
+    n = outer
+    sources, points, length = traces.shape
+    halves, chunks, _, double, width = first_out.shape
+    pieces, piece = model.shape[2], model.shape[5]
+    count = sources // halves
+    depth = n * double
+    block = pieces * piece
+    f32, bf16 = jnp.float32, jnp.bfloat16
+    me, mine = lax.axis_index("gx"), lax.axis_index("ma")
+    core = mine + 1 - 2 * lax.rem(mine, 2)
+    line = lax.rem(mine + 2, 4)
+    corner = lax.rem(core + 2, 4)
+    both = range(halves)
+    sent = summed if mixing else model.at[:, 0]
+
+    def part(i):
+        return pl.ds(pl.multiple_of(i * width, width), width)
+
+    def trace_copy(h, i, s):
+        s = h * count + s
+        return pltpu.make_async_copy(
+            rec_ref.at[part(i), s], traces.at[s, part(i)], trace_sem.at[h, i]
+        )
+
+    def trace_wait(h, i):
+        place = traces.at[h * count : (h + 1) * count, part(i)]
+        pltpu.make_async_copy(place, place, trace_sem.at[h, i]).wait()
+
+    def gain_copy(i):
+        return pltpu.make_async_copy(
+            ker_ref.at[:, part(i)], gains.at[:, part(i)], gain_sem.at[i]
+        )
+
+    kept = (
+        (summed_in, returned_ref),
+        (image_in, imaged_ref),
+        (normal_in, changed_ref),
+        (win, win_ref),
+        (spread, spread_ref),
+        (gather, gather_ref),
+    )
+
+    def keep_copy(number):
+        src, dst = kept[number]
+        return pltpu.make_async_copy(src, dst, keep_sem.at[number])
+
+    def across(number, src, dst, i, peer, slot):
+        return pltpu.make_async_remote_copy(
+            src_ref=src.at[i, peer],
+            dst_ref=dst.at[i, slot],
+            send_sem=out_sem.at[number],
+            recv_sem=in_sem.at[number, i],
+            device_id={"gx": peer},
+            device_id_type=MESH,
+        )
+
+    def send_all(number, h, src, dst, i):
+        src, dst, number = src.at[h], dst.at[h], number * halves + h
+
+        def body(k):
+            peer = lax.rem(me + k, n)
+            across(number, src, dst, i, peer, me).start()
+
+        loop(1, n, body)
+        dst[i, me] = src[i, me]
+
+    def receive_all(number, h, src, dst, i):
+        number = number * halves + h
+        others = pl.ds(0, n - 1)
+        pltpu.make_async_remote_copy(
+            src_ref=src.at[h, i, others],
+            dst_ref=dst.at[h, i, others],
+            send_sem=out_sem.at[number],
+            recv_sem=in_sem.at[number, i],
+            device_id={"gx": lax.rem(me + 1, n)},
+            device_id_type=MESH,
+        ).wait_recv()
+
+    def finish_all(number, src, dst, many):
+        others = pl.ds(0, n - 1)
+        for h in both:
+            pltpu.make_async_remote_copy(
+                src_ref=src.at[h, :, others],
+                dst_ref=dst.at[h, :, others],
+                send_sem=out_sem.at[number * halves + h],
+                recv_sem=in_sem.at[number * halves + h, 0],
+                device_id={"gx": lax.rem(me + 1, n)},
+                device_id_type=MESH,
+            ).wait_send()
+
+    def core_copy(h, stage, which, p):
+        return pltpu.make_async_remote_copy(
+            src_ref=core_out.at[h, stage, which, p],
+            dst_ref=core_in.at[h, stage, which, p],
+            send_sem=core_out_sem,
+            recv_sem=core_in_sem.at[h, stage, which, p],
+            device_id={"ma": core},
+            device_id_type=MESH,
+        )
+
+    def line_copy(h, stage, p):
+        return pltpu.make_async_remote_copy(
+            src_ref=line_out.at[h, stage, p],
+            dst_ref=line_in.at[h, stage, p],
+            send_sem=line_out_sem,
+            recv_sem=line_in_sem.at[h, stage, p],
+            device_id={"ma": line},
+            device_id_type=MESH,
+        )
+
+    def share_copy(h, which, p):
+        source, slot, peer = ((0, 1, core), (0, 2, line), (2, 3, core))[which]
+        return pltpu.make_async_remote_copy(
+            src_ref=model.at[h, source, p],
+            dst_ref=model.at[h, slot, p],
+            send_sem=share_out_sem.at[which],
+            recv_sem=share_in_sem.at[h, which, p],
+            device_id={"ma": peer},
+            device_id_type=MESH,
+        )
+
+    barrier = pltpu.get_barrier_semaphore()
+
+    def greet(k):
+        pl.semaphore_signal(
+            barrier, inc=1, device_id={"gx": lax.rem(me + k, n)}, device_id_type=MESH
+        )
+
+    loop(1, n, greet)
+    for peer in (core, line):
+        pl.semaphore_signal(barrier, inc=1, device_id={"ma": peer}, device_id_type=MESH)
+
+    for h in both:
+        loop(0, chunks, lambda i: loop(0, count, lambda s: trace_copy(h, i, s).start()))
+
+    owners = iota((n, length), 0)
+    bins = jnp.zeros_like(owners)
+    for f in range(n):
+        bins = jnp.where(owners == f, bins_ref[f], bins)
+    angles = lax.rem(bins * iota((n, length), 1), length).astype(f32) * (2.0 * math.pi / length)
+    scale = math.sqrt(2.0 / length)
+    real, imaginary = jnp.cos(angles) * scale, -jnp.sin(angles) * scale
+    rows = []
+    for f in range(n):
+        for values in (real, imaginary):
+            rows.append(jnp.broadcast_to(values[f : f + 1], (count, length)))
+    tall = jnp.concatenate(rows, 0)
+    wide = tall.T
+    row_place = lax.rem(iota((depth, length), 0), count)
+    column_place = lax.rem(iota((length, depth), 1), count)
+    for s in range(count):
+        here = slice(s * length, (s + 1) * length)
+        spread[:, here] = jnp.where(row_place == s, tall, 0.0).astype(bf16)
+        gather[here] = jnp.where(column_place == s, wide, 0.0).astype(bf16)
+    win[:sources] = (1 - start_ref[...]).astype(f32) * (1.0 / RAMP)
+    win[sources:] = stop_ref[...].astype(f32) * (1.0 / RAMP)
+    stats[...] = jnp.zeros_like(stats)
+    if mixing:
+        sides = []
+        for axis in range(2):
+            owner = iota((depth, depth), axis) // double
+            values = jnp.zeros_like(owner)
+            for f in range(n):
+                values = jnp.where(owner == f, bins_ref[f], values)
+            sides.append((values, lax.rem(iota((depth, depth), axis), double)))
+        alike = (sides[0][0] == sides[1][0]) & (sides[0][1] == sides[1][1])
+        same[...] = jnp.where(alike, 1.0, 0.0).astype(bf16)
+    pl.semaphore_wait(barrier, n + 1)
+
+    samples = iota((length, width), 0).astype(f32) * (1.0 / RAMP)
+
+    def span(s, many=1):
+        return pl.ds(pl.multiple_of(s * length, length), many * length)
+
+    def transform(out, h, i):
+        result = jnp.dot(spread[...], tapered[...], preferred_element_type=f32)
+        out[h, i] = result.astype(bf16).reshape(n, double, width)
+
+    def record(h, i):
+        trace_wait(h, i)
+        if h == 0:
+            gain_copy(i).start()
+        for k in range(count):
+            s = h * count + k
+            rising = jnp.clip(samples + win[s : s + 1, part(i)], 0.0, 1.0)
+            falling = jnp.clip(win[sources + s : sources + s + 1, part(i)] - samples, 0.0, 1.0)
+            weight = rising * falling
+            window[i, span(s)] = weight.astype(bf16)
+            tapered[k * length : (k + 1) * length] = (weight * traces[s, part(i)].T).astype(bf16)
+        transform(first_out, h, i)
+        send_all(RECORDED, h, first_out, first_in, i)
+
+    def turned(values, sign):
+        half = double // 2
+        wide_values = values.astype(f32)
+        low, high = wide_values[:, :half], wide_values[:, half:]
+        pair = [high, -low] if sign > 0 else [-high, low]
+        return jnp.concatenate(pair, 1).reshape(depth, values.shape[2]).astype(bf16)
+
+    def adjoint_part(held, h, i, columns):
+        data = held[h, i]
+        return jnp.dot(
+            data.reshape(depth, width), gains[0, part(i), columns], preferred_element_type=f32
+        ) + jnp.dot(turned(data, 1), gains[1, part(i), columns], preferred_element_type=f32)
+
+    rounds = ((RECORDED, first_out, first_in), (SECOND, second_out, second_in))
+
+    def accumulate(stage, h, i):
+        number, src, held = rounds[stage]
+        receive_all(number, h, src, held, i)
+        if stage == 0 and h == 0:
+            gain_copy(i).wait()
+
+        def body(j):
+            columns = pl.ds(pl.multiple_of(j * block, block), block)
+            update = adjoint_part(held, h, i, columns)
+            total[h, :, columns] = update if i == 0 else total[h, :, columns] + update
+
+        loop(0, inner, body)
+
+    last = chunks - 1
+
+    def pack(values):
+        return values.astype(bf16).reshape(n, double, piece)
+
+    def tile(stage, h, where, p):
+        columns = pl.ds(pl.multiple_of(where * block + p * piece, piece), piece)
+        update = adjoint_part(rounds[stage][2], h, last, columns)
+        return update if chunks == 1 else total[h, :, columns] + update
+
+    def from_core(stage, h, which, p):
+        core_copy(h, stage, which, p).wait_recv()
+        return core_in[h, stage, which, p].reshape(depth, piece).astype(f32)
+
+    def reduce_out(stage, h):
+        number, src, held = rounds[stage]
+        receive_all(number, h, src, held, last)
+        if stage == 0 and h == 0:
+            gain_copy(last).wait()
+
+        def to_core(which, where):
+            def body(p):
+                core_out[h, stage, which, p] = pack(tile(stage, h, where, p))
+                core_copy(h, stage, which, p).start()
+
+            loop(0, pieces, body)
+
+        def to_line(p):
+            values = tile(stage, h, line, p)
+            line_out[h, stage, p] = pack(values + from_core(stage, h, 0, p))
+            line_copy(h, stage, p).start()
+
+        to_core(0, corner)
+        loop(0, pieces, to_line)
+        to_core(1, core)
+
+    def reduced(stage, h, p):
+        values = tile(stage, h, mine, p)
+        values = values + from_core(stage, h, 1, p)
+        line_copy(h, stage, p).wait_recv()
+        return pack(values + line_in[h, stage, p].reshape(depth, piece).astype(f32))
+
+    def flat(values):
+        return values.reshape(depth, values.shape[2]).astype(f32)
+
+    def forward_part(h, slot, where, p, rows):
+        columns = pl.ds(pl.multiple_of(where * block + p * piece, piece), piece)
+        values = model[h, slot, p]
+        dims = (((1,), (1,)), ((), ()))
+        return lax.dot_general(
+            gains[0, rows, columns],
+            values.reshape(depth, piece),
+            dims,
+            preferred_element_type=f32,
+        ) + lax.dot_general(
+            gains[1, rows, columns], turned(values, -1), dims, preferred_element_type=f32
+        )
+
+    def forward(h, slot, where, p):
+        tile_rows = 2 * width if chunks % 2 == 0 else width
+
+        def body(i):
+            rows = pl.ds(pl.multiple_of(i * tile_rows, tile_rows), tile_rows)
+            product[h, rows] += forward_part(h, slot, where, p, rows)
+
+        loop(0, points // tile_rows, body)
+
+    def share(h, p):
+        share_copy(h, 1, p).start()
+        share_copy(h, 0, p).start()
+
+    def keep(h, p):
+        values = reduced(0, h, p)
+        if mixing:
+            summed[h, p] = values
+            send_all(RETURNED, h, sent, summed_in, p)
+        else:
+            model[h, 0, p] = values
+            share(h, p)
+            send_all(RETURNED, h, sent, summed_in, p)
+            held = flat(values)
+            stats[0] += folded(held * held)
+
+    def mix(h, p):
+        receive_all(RETURNED, h, sent, summed_in, p)
+        arrived = summed_in[h, p].reshape(depth, piece)
+        values = jnp.dot(same[...], arrived, preferred_element_type=f32)
+        mixed_out[h, p] = values.astype(bf16).reshape(n, double, piece)
+        send_all(MIXED, h, mixed_out, model.at[:, 0], p)
+
+    def unmix(h, p):
+        receive_all(MIXED, h, mixed_out, model.at[:, 0], p)
+        share(h, p)
+
+    def own_forward(h):
+        product[h] = jnp.zeros_like(product[h])
+        loop(0, pieces, lambda p: forward(h, 0, mine, p))
+
+        def from_share(p):
+            share_copy(h, 0, p).wait_recv()
+            forward(h, 1, core, p)
+
+        loop(0, pieces, from_share)
+
+    def relay(h, p):
+        share_copy(h, 1, p).wait_recv()
+        share_copy(h, 2, p).start()
+        forward(h, 2, line, p)
+        share_copy(h, 2, p).wait_recv()
+
+    def from_line(h, p):
+        relay(h, p)
+        forward(h, 3, corner, p)
+
+    final = pieces - 1
+
+    def imaging(h):
+        relay(h, final)
+
+        def body(i):
+            values = product[h, part(i)] + forward_part(h, 3, corner, final, part(i))
+            image_out[h, i] = values.T.astype(bf16).reshape(n, double, width)
+            send_all(IMAGED, h, image_out, image_in, i)
+
+        loop(0, chunks, body)
+
+    def again(h, i):
+        receive_all(IMAGED, h, image_out, image_in, i)
+        arrived = image_in[h, i].reshape(depth, width)
+        for j in range(0, count, GROUP):
+            weight = window[i, span(h * count + j, GROUP)].astype(f32)
+            rows = slice(j * length, (j + GROUP) * length)
+            values = jnp.dot(gather[rows], arrived, preferred_element_type=f32) * weight
+            stats[1] += folded(values * values)
+            tapered[rows] = (values * weight).astype(bf16)
+        transform(second_out, h, i)
+        send_all(SECOND, h, second_out, second_in, i)
+
+    def change(h, p):
+        values = reduced(1, h, p)
+        normal[h, p] = values
+        send_all(CHANGED, h, normal, normal_in, p)
+        if not mixing:
+            held = flat(values)
+            stats[2] += folded(held * flat(model[h, 0, p]))
+            stats[3] += folded(held * held)
+
+    for h in both:
+        loop(0, chunks, lambda i: record(h, i))
+    for number in (3, 4, 5):
+        keep_copy(number).start()
+    for i in range(last):
+        accumulate(0, 0, i)
+    reduce_out(0, 0)
+    for h in both:
+        if h + 1 < halves:
+            for i in range(last):
+                accumulate(0, h + 1, i)
+        loop(0, pieces, lambda p: keep(h, p))
+        if mixing:
+            loop(0, pieces, lambda p: mix(h, p))
+        if h + 1 < halves:
+            reduce_out(0, h + 1)
+        if mixing:
+            loop(0, pieces, lambda p: unmix(h, p))
+        own_forward(h)
+        for p in range(max(chunks, pieces)):
+            if h and p < chunks:
+                again(h - 1, p)
+            if p < final:
+                from_line(h, p)
+        imaging(h)
+    for h in both:
+        for i in range(last):
+            if h:
+                break
+            accumulate(1, h, i)
+        if h == 0:
+            reduce_out(1, h)
+            for p in range(max(chunks, pieces)):
+                if p < chunks:
+                    again(halves - 1, p)
+                if halves > 1 and p < pieces:
+                    change(h, p)
+        else:
+            for i in range(last):
+                accumulate(1, h, i)
+            reduce_out(1, h)
+            loop(0, pieces, lambda p: change(h, p))
+    keep_copy(1).start()
+    if mixing:
+
+        def norms(h, p):
+            receive_all(CHANGED, h, normal, normal_in, p)
+            before = summed_in[h, p].reshape(depth, piece)
+            after = normal_in[h, p].reshape(depth, piece)
+            mixed_before = jnp.dot(same[...], before, preferred_element_type=f32)
+            mixed_after = jnp.dot(same[...], after, preferred_element_type=f32)
+            stats[0] += folded(before.astype(f32) * mixed_before)
+            stats[2] += folded(after.astype(f32) * mixed_before)
+            stats[3] += folded(after.astype(f32) * mixed_after)
+
+        keep_copy(0).start()
+        for h in both:
+            loop(0, pieces, lambda p: norms(h, p))
+    else:
+        for h in both:
+            loop(0, pieces, lambda p: receive_all(RETURNED, h, sent, summed_in, p))
+        keep_copy(0).start()
+
+    def stats_copy(which, src, peer):
+        return pltpu.make_async_remote_copy(
+            src_ref=src,
+            dst_ref=stats_in.at[which],
+            send_sem=stats_out_sem.at[which],
+            recv_sem=stats_in_sem.at[which],
+            device_id={"ma": peer},
+            device_id_type=MESH,
+        )
+
+    def stats_across(peer, slot):
+        return pltpu.make_async_remote_copy(
+            src_ref=stats_in.at[3],
+            dst_ref=stats_all.at[slot],
+            send_sem=stats_out_sem.at[2],
+            recv_sem=stats_in_sem.at[2],
+            device_id={"gx": peer},
+            device_id_type=MESH,
+        )
+
+    to_core = stats_copy(0, stats, core)
+    to_core.start()
+    to_core.wait_recv()
+    stats_in[2] = stats[...] + stats_in[0]
+    to_line = stats_copy(1, stats_in.at[2], line)
+    to_line.start()
+    to_line.wait_recv()
+    stats_in[3] = stats_in[2] + stats_in[1]
+    loop(1, n, lambda k: stats_across(lax.rem(me + k, n), me).start())
+    stats_all[me] = stats_in[3]
+    others = stats_all.at[pl.ds(0, n - 1)]
+    every = pltpu.make_async_remote_copy(
+        src_ref=others,
+        dst_ref=others,
+        send_sem=stats_out_sem.at[2],
+        recv_sem=stats_in_sem.at[2],
+        device_id={"gx": lax.rem(me + 1, n)},
+        device_id_type=MESH,
+    )
+    if not mixing:
+        for h in both:
+            loop(0, pieces, lambda p: receive_all(CHANGED, h, normal, normal_in, p))
+    keep_copy(2).start()
+    every.wait_recv()
+    sums_ref[...] = jnp.sum(stats_all[...], axis=0)
+
+    to_core.wait_send()
+    to_line.wait_send()
+    every.wait_send()
+    finish_all(RECORDED, first_out, first_in, chunks)
+    finish_all(RETURNED, sent, summed_in, pieces)
+    finish_all(IMAGED, image_out, image_in, chunks)
+    finish_all(SECOND, second_out, second_in, chunks)
+    finish_all(CHANGED, normal, normal_in, pieces)
+    if mixing:
+        finish_all(MIXED, mixed_out, model.at[:, 0], pieces)
+
+    def finish(src, dst, sem, peer):
+        pltpu.make_async_remote_copy(
+            src_ref=src,
+            dst_ref=dst,
+            send_sem=sem,
+            recv_sem=stats_in_sem.at[0],
+            device_id={"ma": peer},
+            device_id_type=MESH,
+        ).wait_send()
+
+    finish(core_out, core_in, core_out_sem, core)
+    finish(line_out, line_in, line_out_sem, line)
+    for which, peer in ((0, core), (1, line), (2, core)):
+        finish(model.at[:, 0], model.at[:, 1], share_out_sem.at[which], peer)
+    for number in range(6):
+        keep_copy(number).wait()
+
+
+def iteration(outer, inner, mixing, freq_bins, recorded, kernel, window_start, window_stop):
+    points, sources, length = recorded.shape
+    columns = kernel.shape[2]
+    halves = PARTS
+    count = sources // halves
+    double = 2 * count
+    depth = outer * double
+    block = columns // inner
+    width, piece = min(256, points), min(256, block)
+    chunks, pieces = points // width, block // piece
+    f32, bf16 = jnp.float32, jnp.bfloat16
+    by_chunk = (halves, chunks, outer, double, width)
+    by_piece = (halves, pieces, outer, double, piece)
+    stack = by_piece[1:]
+    vmem = pl.BlockSpec(memory_space=pltpu.VMEM)
+    hbm = pl.BlockSpec(memory_space=pl.ANY)
+    dma = pltpu.SemaphoreType.DMA
+    exchanges = 6 if mixing else 5
+    extra = by_piece if mixing else (halves, 1, 1, 16, 128)
+    return pl.pallas_call(
+        functools.partial(iteration_kernel, outer, inner, mixing),
+        out_shape=[
+            jax.ShapeDtypeStruct(by_piece, bf16),
+            jax.ShapeDtypeStruct(by_chunk, bf16),
+            jax.ShapeDtypeStruct(by_piece, bf16),
+            jax.ShapeDtypeStruct((4, 8, 128), f32),
+            jax.ShapeDtypeStruct((2 * sources, points), f32),
+            jax.ShapeDtypeStruct((depth, count * length), bf16),
+            jax.ShapeDtypeStruct((count * length, depth), bf16),
+        ],
+        in_specs=[pl.BlockSpec(memory_space=pltpu.SMEM), hbm, hbm, vmem, vmem],
+        out_specs=[hbm, hbm, hbm, vmem, hbm, hbm, hbm],
+        scratch_shapes=[
+            pltpu.VMEM((sources, points, length), f32),
+            pltpu.VMEM((2, points, columns), bf16),
+            pltpu.VMEM((chunks, sources * length, width), bf16),
+            pltpu.VMEM((2 * sources, points), f32),
+            pltpu.VMEM((depth, count * length), bf16),
+            pltpu.VMEM((count * length, depth), bf16),
+            pltpu.VMEM((count * length, width), bf16),
+            pltpu.VMEM(by_chunk, bf16),
+            pltpu.VMEM(by_chunk, bf16),
+            pltpu.VMEM(by_chunk, bf16),
+            pltpu.VMEM(by_chunk, bf16),
+            pltpu.VMEM((halves, depth, columns), f32),
+            pltpu.VMEM((halves, points, depth), f32),
+            pltpu.VMEM(by_chunk, bf16),
+            pltpu.VMEM(by_chunk, bf16),
+            pltpu.VMEM((halves, 2, 2) + stack, bf16),
+            pltpu.VMEM((halves, 2, 2) + stack, bf16),
+            pltpu.VMEM((halves, 2) + stack, bf16),
+            pltpu.VMEM((halves, 2) + stack, bf16),
+            pltpu.VMEM((halves, 4) + stack, bf16),
+            pltpu.VMEM(extra, bf16),
+            pltpu.VMEM(by_piece, bf16),
+            pltpu.VMEM(by_piece, bf16),
+            pltpu.VMEM(by_piece, bf16),
+            pltpu.VMEM(extra, bf16),
+            pltpu.VMEM((depth, depth) if mixing else (16, 128), bf16),
+            pltpu.VMEM((4, 8, 128), f32),
+            pltpu.VMEM((4, 4, 8, 128), f32),
+            pltpu.VMEM((outer, 4, 8, 128), f32),
+            dma((halves, chunks)),
+            dma((chunks,)),
+            dma((6,)),
+            dma((exchanges * halves,)),
+            dma((exchanges * halves, max(chunks, pieces))),
+            dma,
+            dma((halves, 2, 2, pieces)),
+            dma,
+            dma((halves, 2, pieces)),
+            dma((3,)),
+            dma((halves, 3, pieces)),
+            dma((3,)),
+            dma((3,)),
+        ],
+        compiler_params=pltpu.CompilerParams(
+            collective_id=6 if mixing else 5,
+            has_side_effects=True,
+            vmem_limit_bytes=67_000_000,
+        ),
+        name="iteration_mixed" if mixing else "iteration",
+    )(freq_bins, recorded, kernel, window_start, window_stop)
+
+
+def write_kernel(
+    sums_ref, rec_ref, win_ref, spread_ref, gather_ref, ret_ref, ima_ref, cha_ref,
+    sol_ref, res_ref, dir_ref, traces, solved, rest, ahead, in_sem, out_sem,
+):
+    sources, points, length = traces.shape
+    halves, chunks, outer, double, width = ima_ref.shape
+    depth = outer * double
+    count = sources // halves
+    f32, bf16 = jnp.float32, jnp.bfloat16
+
+    def part(i):
+        return pl.ds(pl.multiple_of(i * width, width), width)
+
+    def load(i, s):
+        return pltpu.make_async_copy(
+            rec_ref.at[part(i), s], traces.at[s, part(i)], in_sem.at[i]
+        )
+
+    staged = ((solved, sol_ref), (ahead, dir_ref), (rest, res_ref))
+
+    def store(number, i, s):
+        src, dst = staged[number]
+        return pltpu.make_async_copy(
+            src.at[s, part(i)], dst.at[part(i), s], out_sem.at[number]
+        )
+
+    loop(0, chunks, lambda i: loop(0, sources, lambda s: load(i, s).start()))
+    norm_start, norm_data = jnp.sum(sums_ref[0]), jnp.sum(sums_ref[1])
+    cross, norm_change = jnp.sum(sums_ref[2]), jnp.sum(sums_ref[3])
+    step_size = norm_start / (norm_data + epsilon)
+    norm_final = norm_start - 2.0 * step_size * cross + step_size * step_size * norm_change
+    ratio = norm_final / (norm_start + epsilon)
+    samples = iota((length, width), 0).astype(f32) * (1.0 / RAMP)
+
+    def chunk(i):
+        place = traces.at[:, part(i)]
+        pltpu.make_async_copy(place, place, in_sem.at[i]).wait()
+        for h in range(halves):
+            before = ret_ref[h, i].reshape(depth, width).astype(f32).T.astype(bf16)
+            after = cha_ref[h, i].reshape(depth, width).astype(f32).T.astype(bf16)
+            arrived = ima_ref[h, i].reshape(depth, width)
+
+            def pair(j):
+                spans = pl.ds(pl.multiple_of(j * 2 * length, length), 2 * length)
+                table = spread_ref[:, spans]
+                first = h * count + 2 * j
+                for r in range(0, width, 128):
+                    rows = pl.ds(pl.multiple_of(i * width + r, 128), 128)
+                    gradient = jnp.dot(before[r : r + 128], table, preferred_element_type=f32)
+                    change = jnp.dot(after[r : r + 128], table, preferred_element_type=f32)
+                    for k in range(2):
+                        here = slice(k * length, (k + 1) * length)
+                        g, c = gradient[:, here], change[:, here]
+                        solved[first + k, rows] = step_size * g
+                        ahead[first + k, rows] = (g - step_size * c) + ratio * g
+                for k in range(2):
+                    s = first + k
+                    store(0, i, s).start()
+                    store(1, i, s).start()
+                    rising = jnp.clip(samples + win_ref[pl.ds(s, 1), part(i)], 0.0, 1.0)
+                    falling = jnp.clip(
+                        win_ref[pl.ds(sources + s, 1), part(i)] - samples, 0.0, 1.0
+                    )
+                    spans = pl.ds(pl.multiple_of((2 * j + k) * length, length), length)
+                    image = jnp.dot(gather_ref[spans], arrived, preferred_element_type=f32)
+                    image = (rising * falling) * image
+                    rest[s, part(i)] = traces[s, part(i)] - step_size * image.T
+                    store(2, i, s).start()
+
+            loop(0, count // 2, pair)
+
+    loop(0, chunks, chunk)
+    for number in range(3):
+        src = staged[number][0]
+        pltpu.make_async_copy(src, src, out_sem.at[number]).wait()
+
+
+def write(recorded, returned, imaged, changed, sums, windows, spread, gather):
+    points, sources, length = recorded.shape
+    halves, chunks, outer, double, width = imaged.shape
+    depth = outer * double
+    vmem = pl.BlockSpec(memory_space=pltpu.VMEM)
+    hbm = pl.BlockSpec(memory_space=pl.ANY)
+    f32 = jnp.float32
+    staged = pltpu.VMEM((sources, points, length), f32)
+    return pl.pallas_call(
+        write_kernel,
+        out_shape=[jax.ShapeDtypeStruct(recorded.shape, f32)] * 3,
+        in_specs=[vmem, hbm] + [vmem] * 6,
+        out_specs=[hbm] * 3,
+        scratch_shapes=[
+            staged,
+            staged,
+            staged,
+            staged,
+            pltpu.SemaphoreType.DMA((chunks,)),
+            pltpu.SemaphoreType.DMA((3,)),
+        ],
+        compiler_params=pltpu.CompilerParams(vmem_limit_bytes=56 * 1024 * 1024),
+        cost_estimate=pl.CostEstimate(
+            flops=6 * points * sources * depth * length,
+            bytes_accessed=16 * points * sources * length,
+            transcendentals=0,
+        ),
+        name="write",
+    )(sums, recorded, windows, spread, gather, returned, imaged, changed)
+
+
+def fused(outer, inner, recorded, kernel, freq_bins, window_start, window_stop):
+    same = freq_bins[:, None] == freq_bins[None, :]
+    repeated = jnp.sum(same.astype(jnp.int32)) > freq_bins.shape[0]
+    gains = kernel.reshape(2, kernel.shape[2], kernel.shape[3])
+    results = lax.cond(
+        repeated,
+        lambda *x: tuple(iteration(outer, inner, True, *x)),
+        lambda *x: tuple(iteration(outer, inner, False, *x)),
+        freq_bins, recorded, gains, window_start.T, window_stop.T,
+    )
+    return tuple(write(recorded, *results))
+
+
+def fits(outer, inner, recorded, kernel):
+    points, sources, length = recorded.shape
+    columns = kernel.shape[3]
+    return (
+        inner == 4
+        and kernel.shape[1] == 1
+        and columns == inner * points
+        and sources % (PARTS * 8) == 0
+        and length % 128 == 0
+        and points % 256 == 0
+        and outer * 2 * (sources // PARTS) % 128 == 0
+        and points * (4 * columns + 6 * sources * length) < 30_000_000
+    )
+
+
 def per_device(outer, inner, recorded, kernel, freq_bins, window_start, window_stop):
+    if fits(outer, inner, recorded, kernel):
+        return fused(outer, inner, recorded, kernel, freq_bins, window_start, window_stop)
     length = recorded.shape[2]
     table = phase_table(freq_bins, length)
     weights = taper_weights(window_start, window_stop, length)

time: 239 us -> 117 us (0.49)
  waiting for transfers between devices: 40 us -> 0 us
  matrix products: 33.4 us -> 0 us
  local copies, waits for them, and re-layouts: 18.4 us -> 0 us
  starting transfers between devices: 12.4 us -> 0 us
  other arithmetic: 13.6 us -> 1.44 us
  Pallas kernels: 117 us -> 114 us
    dot_general x6 -> x0, matrix products: 33.4 us -> none  [the longest x2 14.9 us: to_spectra(): jnp.einsum('ast,kt->ksa', traces.astype(jnp.bfloat16), flat, preferred_el...]
    ppermute x6 -> x0, waiting for transfers between devices: 29.9 us -> none  [the longest x4 15.4 us: scatter_sum(): got = lax.ppermute(send, 'ma', pairs(n, bit))]
    all_to_all x1 -> x0, waiting for transfers between devices: 10.1 us -> none  [per_device(): lax.all_to_all(by_source(adjoint, outer), 'gx', split_axis=0, concat_axis...]
    all_to_all x1 -> x0, starting transfers between devices: 7.57 us -> none  [per_device(): lax.all_to_all(by_source(adjoint, outer), 'gx', split_axis=0, concat_axis...]
    convert_element_type x11 -> x0, other arithmetic: 6.75 us -> none  [the longest x4 5.01 us: scatter_sum(): (keep.astype(jnp.float32) + got.astype(jnp.float32)).astype(jnp.bfloat16)]
    reshape x5 -> x0, local copies, waits for them, and re-layouts: 6.45 us -> none  [the longest x2 3.76 us: by_frequency(): arrived.reshape(n, 2, sources, points).transpose(1, 0, 2, 3)]
    ppermute x6 -> x0, starting transfers between devices: 4.83 us -> none  [the longest x4 3.24 us: scatter_sum(): got = lax.ppermute(send, 'ma', pairs(n, bit))]
    another operation x6 -> x0, other arithmetic: 4.02 us -> none  [the longest x1 2.63 us: per_device(): jnp.stack([jnp.sum(flat_g.astype(jnp.float32) * mixed_g), jnp.sum(image *...]
  transfers between devices with their start and end apart: 7 -> 0, of which waited for: 6 -> 0; matrix products, arithmetic and copies ran while one was open for 2% -> 0% of each run, Pallas kernels for 0% -> 0%
where the time goes in v2:
time: 117 us
  Pallas kernels  114 us (97%)
  between operations  1.45 us (1%)
  other arithmetic  1.44 us (1%)
    pallas_call x1, Pallas kernels, iteration(): pl.pallas_call(functools.partial(iteration_kernel, outer, inner, mixing),...  97 us
    pallas_call x1, Pallas kernels, write(): pl.pallas_call(write_kernel, out_shape=[jax.ShapeDtypeStruct(recorded.sha...  16.9 us

profile of v2, /device:TPU:0, one launch (start us, length us, event | category | flops | bytes accessed | tf_op | source)
XLA Modules:
  0.0 117.0 jit_solution(14679666930570128305)
XLA Ops:
  0.6 1.4 %convert_reduce_fusion = s32[]{:T(128)} fusion(s32[8]{0:T(128)} %param.9), kind=kLoop, calls=%fused_computation | loop fusion | flops 191 | bytes 36 | tf_op jit(solution)/shard_map/reduce_sum | solution.py:1064
  2.7 97.2 %conditional.1 = ((bf16[2,4,8,16,256]{4,3,2,1,0:T(8,128)(2,1)}, bf16[2,4,8,16,256]{4,3,2,1,0:T(8,128)(2,1)}, bf16[2,4,8,16,256]{4,3,2,1,0:T(8,128)(2,1)}, f32[4,...) conditional(s32[]{:T(128)} %convert_element_type.7, ...), branch_computations={%region_1.0_spmd, %region_2.0_spmd} | conditional | bytes 8 | solution.py:1066
  2.7 97.0 %iteration.1 = (bf16[2,4,8,16,256]{4,3,2,1,0:T(8,128)(2,1)}, bf16[2,4,8,16,256]{4,3,2,1,0:T(8,128)(2,1)}, bf16[2,4,8,16,256]{4,3,2,1,0:T(8,128)(2,1)}, f32[4,8,1...) custom-call(s32[8]{0:T(128)} %get-tuple-element.20.bins_ref, ...), custom_call_target="tpu_custom_call" | custom-call | tf_op jit(solution)/shard_map/cond/branch_0_fun/iteration/pallas_call | solution.py:888
  99.9 16.9 %write.1 = (f32[1024,16,128]{2,1,0:T(8,128)}, f32[1024,16,128]{2,1,0:T(8,128)}, f32[1024,16,128]{2,1,0:T(8,128)}) custom-call(f32[4,8,128]{2,1,0:T(8,128)S(1)} %get-tuple-element.40.sums_ref, f32[1024,16,128]{2,1,0:T(8,128)} %rec_ref.1, f32[32,1024]{1,0:T(8,128)} %get-tuple-element.41.win_ref, bf16[128,1024]{1,0:T(8,128)(2,1)} %get-tuple-element.42.spread_ref, ...), custom_call_target="tpu_custom_call" | custom-call | flops 1610612736 | bytes 33554432 | tf_op jit(solution)/shard_map/write/pallas_call | solution.py:1039
